TPU v7x, 8 devices: a whole 2x2x1 slice. The times are simulated.
8 devices in a mesh: dp: 1 (over z), tp: 2 (over y), sp: 4 (over x, core).
Axes of the slice: x: 2, y: 2, z: 1, core: 2. Of those that a mesh axis runs over, the one named last changes fastest.
Arguments:
- tokens: bfloat16 [8192, 4096], P(('dp', 'sp'))
- glob_pos: int32 [512], P('dp')
- w_query: bfloat16 [4096, 32, 128], P(None, 'tp')
- w_key: bfloat16 [4096, 32, 128], P(None, 'tp')
- w_value: bfloat16 [4096, 32, 128], P(None, 'tp')
- w_out: bfloat16 [32, 128, 4096], P('tp')
- w_up: bfloat16 [4096, 14336], P(None, 'tp')
- w_down: bfloat16 [14336, 4096], P('tp')
Outputs:
- output: bfloat16 [8192, 4096], P(('dp', 'sp'))
All inputs are finite; a program needn't handle non-finite values.
Results may differ from a plain program's by a relative error of at most 0.0118318.
Values are sent between devices in bfloat16 or wider.
A program may use at most 1 GiB of HBM per device.

v0:
```python
import jax
import jax.numpy as jnp
from jax import lax
from jax.sharding import PartitionSpec as P
import math

WIN = 256


def local_window(q_rows, k_ext, v_ext, k_glob, v_glob, glob_pos, first_row, seq_len):
    n_rows, n_heads, head_dim = q_rows.shape
    scale = 1.0 / math.sqrt(head_dim)
    q_block = 128
    key_span = q_block + 2 * WIN

    def one_block(blk_index):
        start = blk_index * q_block
        q_blk = lax.dynamic_slice_in_dim(q_rows, start, q_block)
        k_blk = lax.dynamic_slice_in_dim(k_ext, start, key_span)
        v_blk = lax.dynamic_slice_in_dim(v_ext, start, key_span)
        q_pos = first_row + start + jnp.arange(q_block)
        k_pos = first_row + start - WIN + jnp.arange(key_span)
        k_is_glob = jnp.any(k_pos[:, None] == glob_pos[None, :], axis=1)
        k_ok = (k_pos >= 0) & (k_pos < seq_len) & jnp.logical_not(k_is_glob)
        allowed = (jnp.abs(q_pos[:, None] - k_pos[None, :]) <= WIN) & k_ok[None, :]
        s_win = jnp.einsum('qhe,khe->hqk', q_blk, k_blk, preferred_element_type=jnp.float32) * scale
        s_win = jnp.where(allowed[None], s_win, -jnp.inf)
        s_glob = jnp.einsum('qhe,ghe->hqg', q_blk, k_glob, preferred_element_type=jnp.float32) * scale
        row_max = jnp.maximum(jnp.max(s_win, axis=2, keepdims=True), jnp.max(s_glob, axis=2, keepdims=True))
        e_win = jnp.exp(s_win - row_max)
        e_glob = jnp.exp(s_glob - row_max)
        total = jnp.sum(e_win, axis=2, keepdims=True) + jnp.sum(e_glob, axis=2, keepdims=True)
        p_win = (e_win / total).astype(jnp.bfloat16)
        p_glob = (e_glob / total).astype(jnp.bfloat16)
        blk_out = jnp.einsum('hqk,khe->qhe', p_win, v_blk, preferred_element_type=jnp.float32)
        blk_out = blk_out + jnp.einsum('hqg,ghe->qhe', p_glob, v_glob, preferred_element_type=jnp.float32)
        return blk_out.astype(jnp.bfloat16)

    blocks = lax.map(one_block, jnp.arange(n_rows // q_block))
    return blocks.reshape(n_rows, n_heads, head_dim)


def pick_rows(row_array, safe_idx, owned):
    picked = jnp.take(row_array, safe_idx, axis=0)
    return jnp.where(owned[:, None, None], picked, 0)


def global_queries(q_glob, k_rows, v_rows):
    scale = 1.0 / math.sqrt(q_glob.shape[2])
    scores = jnp.einsum('ghe,rhe->hgr', q_glob, k_rows, preferred_element_type=jnp.float32) * scale
    glob_max = lax.pmax(jnp.max(scores, axis=2, keepdims=True), 'sp')
    exp_scores = jnp.exp(scores - glob_max)
    glob_sum = lax.psum(jnp.sum(exp_scores, axis=2, keepdims=True), 'sp')
    prob_rows = (exp_scores / glob_sum).astype(jnp.bfloat16)
    part_out = jnp.einsum('hgr,rhe->ghe', prob_rows, v_rows, preferred_element_type=jnp.float32)
    return lax.psum(part_out, 'sp').astype(jnp.bfloat16)


def solution(mesh):
    n_seq = mesh.shape['sp']
    to_right = [(i, i + 1) for i in range(n_seq - 1)]
    to_left = [(i + 1, i) for i in range(n_seq - 1)]

    def device_layer(tokens, glob_pos, w_query, w_key, w_value, w_out, w_up, w_down):
        n_rows = tokens.shape[0]
        first_row = lax.axis_index('sp') * n_rows
        q_rows = jnp.einsum('rd,dhe->rhe', tokens, w_query, preferred_element_type=jnp.float32).astype(jnp.bfloat16)
        k_rows = jnp.einsum('rd,dhe->rhe', tokens, w_key, preferred_element_type=jnp.float32).astype(jnp.bfloat16)
        v_rows = jnp.einsum('rd,dhe->rhe', tokens, w_value, preferred_element_type=jnp.float32).astype(jnp.bfloat16)
        left_k, left_v = lax.ppermute((k_rows[n_rows - WIN:], v_rows[n_rows - WIN:]), 'sp', to_right)
        right_k, right_v = lax.ppermute((k_rows[:WIN], v_rows[:WIN]), 'sp', to_left)
        k_ext = jnp.concatenate([left_k, k_rows, right_k], axis=0)
        v_ext = jnp.concatenate([left_v, v_rows, right_v], axis=0)
        local_idx = glob_pos - first_row
        owned = (local_idx >= 0) & (local_idx < n_rows)
        safe_idx = jnp.clip(local_idx, 0, n_rows - 1)
        picked = (pick_rows(q_rows, safe_idx, owned), pick_rows(k_rows, safe_idx, owned), pick_rows(v_rows, safe_idx, owned))
        q_glob, k_glob, v_glob = lax.psum(picked, 'sp')
        attn_rows = local_window(q_rows, k_ext, v_ext, k_glob, v_glob, glob_pos, first_row, n_rows * n_seq)
        glob_out = global_queries(q_glob, k_rows, v_rows)
        attn_rows = attn_rows.at[jnp.where(owned, local_idx, n_rows)].set(glob_out, mode='drop')
        mixed = lax.psum(jnp.einsum('rhe,hed->rd', attn_rows, w_out, preferred_element_type=jnp.float32), 'tp')
        hidden = (tokens.astype(jnp.float32) + mixed).astype(jnp.bfloat16)
        gelu_rows = jax.nn.gelu(jnp.dot(hidden, w_up, preferred_element_type=jnp.float32), approximate=True).astype(jnp.bfloat16)
        down_sum = lax.psum(jnp.dot(gelu_rows, w_down, preferred_element_type=jnp.float32), 'tp')
        return (hidden.astype(jnp.float32) + down_sum).astype(jnp.bfloat16)

    row_spec = P(('dp', 'sp'), None)
    head_spec = P(None, 'tp', None)
    in_specs = (row_spec, P('dp'), head_spec, head_spec, head_spec, P('tp', None, None), P(None, 'tp'), P('tp', None))
    return jax.shard_map(device_layer, mesh=mesh, in_specs=in_specs, out_specs=row_spec, check_vma=False)
```

profile of v0, /device:TPU:0, one launch (start us, length us, event | category | flops | bytes accessed | tf_op | source)
XLA Modules:
  0.0 2691.6 jit_solution(11715831888234397709)
XLA Ops:
  8.4 42.6 %fusion.67 = bf16[2048,16,128]{2,0,1:T(8,128)(2,1)} fusion(bf16[4096,16,128]{2,1,0:T(8,128)(2,1)} %param.15, bf16[2048,4096]{1,0:T(8,128)(2,1)} %param.12), kind=kOutput, calls=%fused_computation.75 | convolution fusion | flops 34363932672 | bytes 41943040 | tf_op jit(solution)/shard_map/rd,dhe->rhe/dot_general | solution.py:68
  51.0 42.8 %fusion.57 = bf16[2048,16,128]{2,0,1:T(8,128)(2,1)} fusion(bf16[4096,16,128]{2,1,0:T(8,128)(2,1)} %param.16, bf16[2048,4096]{1,0:T(8,128)(2,1)} %param.12), kind=kOutput, calls=%fused_computation.73 | convolution fusion | flops 34363932672 | bytes 41943040 | tf_op jit(solution)/shard_map/rd,dhe->rhe/dot_general | solution.py:69
  93.8 42.8 %fusion.62 = bf16[2048,16,128]{2,0,1:T(8,128)(2,1)} fusion(bf16[4096,16,128]{2,1,0:T(8,128)(2,1)} %param.14, bf16[2048,4096]{1,0:T(8,128)(2,1)} %param.12), kind=kOutput, calls=%fused_computation.74 | convolution fusion | flops 34363932672 | bytes 41943040 | tf_op jit(solution)/shard_map/rd,dhe->rhe/dot_general | solution.py:67
  136.6 10.6 copy.39
  147.2 24.4 copy.35
  171.6 4.6 gather_fusion.2
  176.2 5.8 gather_fusion.1
  182.0 10.3 copy.33
  192.4 5.7 gather_fusion
  198.1 7.5 fusion.73
  205.6 3.1 fusion.83
  208.7 2.8 collective-permute-start
  213.0 3.1 fusion.82
  216.2 5.1 collective-permute-start.2
  223.2 11.4 pad_maximum_fusion
  234.7 8.0 pad_maximum_fusion.1
  242.7 102.2 %all-reduce.10.cloned.1.call-done = (bf16[512,16,128]{2,0,1:T(8,128)(2,1)}, bf16[512,16,128]{2,0,1:T(8,128)(2,1)}, bf16[512,16,128]{2,0,1:T(8,128)(2,1)}) async-done(((bf16[512,16,128]{2,0,1:T(8,128)(2,1)}, bf16[512,16,128]{2,0,1:T(8,128)(2,1)}, bf16[512,16,128]{2,0,1:T(8,128)(2,1)}), (bf16[512,16,128]{2,0,1:T(8,128)(2,1)}, bf16[512,16,128]{2,0,1:T(8,128)(2,1)}, ...) | async-done | bytes 6291472 | tf_op jit(solution)/shard_map/psum | solution.py:78
  344.9 288.5 %while.12 = (s32[]{:T(128)}, bf16[16,128,16,128]{3,2,1,0:T(8,128)(2,1)}, s32[16]{0:T(128)S(1)}, bf16[2560,16,128]{2,0,1:T(8,128)(2,1)}, s32[]{:T(128)}, /*index=...) while((s32[]{:T(128)}, ...), condition=%wide.region_8.10_spmd, body=%wide.region_2.9_spmd.sunk | while | flops 1234632576 | bytes 52376900 | solution.py:39
  349.2 3.2 fusion.109
  357.6 4.0 fusion.113
  367.3 3.2 fusion.109
  375.7 4.0 fusion.113
  385.3 3.2 fusion.109
  393.7 4.0 fusion.113
  403.3 3.2 fusion.109
  411.7 4.0 fusion.113
  421.4 3.2 fusion.109
  429.8 4.0 fusion.113
  439.4 3.2 fusion.109
  447.8 4.0 fusion.113
  457.5 3.2 fusion.109
  465.9 4.0 fusion.113
  475.5 3.2 fusion.109
  483.9 4.0 fusion.113
  493.5 3.2 fusion.109
  501.9 4.0 fusion.113
  511.5 3.2 fusion.109
  519.9 4.0 fusion.113
  529.5 3.2 fusion.109
  537.9 4.0 fusion.113
  547.6 3.2 fusion.109
  556.0 4.0 fusion.113
  565.6 3.2 fusion.109
  574.0 4.0 fusion.113
  583.6 3.2 fusion.109
  592.0 4.0 fusion.113
  601.7 3.2 fusion.109
  610.1 4.0 fusion.113
  619.7 3.2 fusion.109
  628.1 4.0 fusion.113
  633.4 26.7 multiply_reduce_fusion.1
  660.1 10.4 pmax.7
  670.6 21.2 fusion.39
  691.8 10.6 psum.52
  702.5 30.7 %fusion.72 = f32[512,16,128]{0,2,1:T(8,128)} fusion(bf16[2048,16,128]{2,0,1:T(8,128)(2,1)} %fusion.57, f32[16,512,2048]{2,1,0:T(8,128)} %get-tuple-element.200, f32[16,512]{1,0:T(8,128)S(1)} %psum.52, f32[16,512]{1,0:T(8,128)S(1)} %pmax.7), kind=kOutput, calls=%fused_computation.76 | convolution fusion | flops 4362076160 | bytes 79757312 | tf_op jit(solution)/shard_map/hgr,rhe->ghe/dot_general | solution.py:55
  733.1 76.4 %all-reduce.11 = bf16[512,16,128]{0,2,1:T(8,128)(2,1)S(1)} all-reduce(f32[512,16,128]{0,2,1:T(8,128)} %fusion.72), channel_id=1, replica_groups=mesh['dp'=1,'tp'=2,'sp'=4] {'sp'}, use_global_device_ids=true, to_apply=%region_14.16 | all-reduce | flops 1048576 | bytes 6291456 | tf_op jit(solution)/shard_map/psum | solution.py:56
  809.5 3.1 copy.42
  812.6 45.7 %scatter_fusion = bf16[2048,16,128]{2,1,0:T(8,128)(2,1)} fusion(bf16[2048,16,128]{2,1,0:T(8,128)(2,1)} %bitcast.56, s32[512]{0:T(512)S(1)} %copy-done.4, bf16[512,16,128]{2,1,0:T(8,128)(2,1)} %copy.42), kind=kCustom, calls=%fused_computation.3 | custom fusion | bytes 6293504 | tf_op jit(solution)/shard_map/scatter | solution.py:81
  858.3 42.9 %convolution_bitcast_fusion = f32[2048,4096]{1,0:T(8,128)} fusion(bf16[16,128,4096]{2,1,0:T(8,128)(2,1)} %param.17, bf16[2048,16,128]{2,1,0:T(8,128)(2,1)} %scatter_fusion), kind=kOutput, calls=%fused_computation.60 | convolution fusion | flops 34359738368 | bytes 58720256 | tf_op jit(solution)/shard_map/rhe,hed->rd/dot_general | solution.py:82
  901.3 733.5 %all-reduce.6.cloned.1.call-done = f32[2048,4096]{1,0:T(8,128)} async-done(((f32[2048,4096]{1,0:T(8,128)}), f32[2048,4096]{1,0:T(8,128)}) %all-reduce.6.cloned.1.call-update) | async-done | bytes 33554448 | tf_op jit(solution)/shard_map/psum | solution.py:82
  1634.7 142.6 %fusion.81 = f32[2048,7168]{1,0:T(8,128)} fusion(bf16[4096,7168]{1,0:T(8,128)(2,1)} %param.18, f32[2048,4096]{1,0:T(8,128)} %all-reduce.6.cloned.1.call-done, bf16[2048,4096]{1,0:T(8,128)(2,1)} %param.12), kind=kOutput, calls=%fused_computation.93 | convolution fusion | flops 120284250112 | bytes 167772160 | tf_op jit(solution)/shard_map/dot_general | solution.py:84
  1777.4 141.2 %fusion.41 = f32[2048,4096]{1,0:T(8,128)} fusion(bf16[7168,4096]{1,0:T(8,128)(2,1)} %param.19, f32[2048,7168]{1,0:T(8,128)} %fusion.81), kind=kOutput, calls=%fused_computation.55 | convolution fusion | flops 120391204864 | bytes 150994944 | tf_op jit(solution)/shard_map/dot_general | solution.py:85
  1918.7 733.4 %all-reduce.8.cloned.1.call-done = f32[2048,4096]{1,0:T(8,128)} async-done(((f32[2048,4096]{1,0:T(8,128)}), f32[2048,4096]{1,0:T(8,128)}) %all-reduce.8.cloned.1.call-update) | async-done | bytes 33554448 | tf_op jit(solution)/shard_map/psum | solution.py:85
  2652.0 32.6 %add_convert_fusion = bf16[2048,4096]{1,0:T(8,128)(2,1)} fusion(f32[2048,4096]{1,0:T(8,128)} %all-reduce.8.cloned.1.call-done, f32[2048,4096]{1,0:T(8,128)} %all-reduce.6.cloned.1.call-done, bf16[2048,4096]{1,0:T(8,128)(2,1)} %param.12), kind=kLoop, calls=%fused_computation.52 | loop fusion | flops 50331648 | bytes 100663296 | tf_op jit(solution)/shard_map/convert_element_type | solution.py:86
  (292 shorter events, 165.7 us)
Async XLA Ops:
  6.5 338.4 %all-reduce.10.cloned.1.call-start = ((), (), s32[]{:S(2)}) async-start(), calls=%async_computation.2 | async-start | bytes 12582912 | tf_op jit(solution)/shard_map/psum | solution.py:78
  136.6 10.6 copy-start
  147.2 24.4 copy-start.3
  182.0 16.1 copy-start.5
  182.0 16.1 copy-start.6
  205.6 17.0 copy-start.2
  205.6 1429.2 %all-reduce.6.cloned.1.call-start = ((), (), s32[]{:S(2)}) async-start(), calls=%async_computation | async-start | bytes 67108864 | tf_op jit(solution)/shard_map/psum | solution.py:82
  208.7 14.5 collective-permute-start
  211.6 11.7 collective-permute-start.1
  216.2 18.5 collective-permute-start.2
  221.3 13.4 collective-permute-start.3
  222.6 12.0 slice-start
  223.2 11.5 slice-start.1
  344.9 288.5 %copy-start.1 = (bf16[512,16,128]{2,0,1:T(8,128)(2,1)S(1)}, bf16[512,16,128]{2,0,1:T(8,128)(2,1)}, u32[]{:S(2)}) copy-start(bf16[512,16,128]{2,0,1:T(8,128)(2,1)} %get-tuple-element.184) | copy-start | bytes 6291460
  349.2 6.0 copy-start.7
  367.3 6.0 copy-start.7
  385.3 6.0 copy-start.7
  403.3 6.0 copy-start.7
  421.4 6.0 copy-start.7
  439.4 6.0 copy-start.7
  457.4 6.0 copy-start.7
  475.5 6.0 copy-start.7
  493.5 6.0 copy-start.7
  511.5 6.0 copy-start.7
  529.5 6.0 copy-start.7
  547.6 6.0 copy-start.7
  565.6 6.0 copy-start.7
  583.6 6.0 copy-start.7
  601.7 6.0 copy-start.7
  619.7 6.0 copy-start.7
  733.1 79.4 %copy-start.4 = (s32[512]{0:T(512)S(1)}, s32[512]{0:T(512)}, u32[]{:S(2)}) copy-start(s32[512]{0:T(512)} %compare_select_fusion.1) | copy-start | bytes 6148
  901.2 1750.8 %all-reduce.8.cloned.1.call-start = ((), (), s32[]{:S(2)}) async-start(), calls=%async_computation.1 | async-start | bytes 67108864 | tf_op jit(solution)/shard_map/psum | solution.py:85
Sparse Core Ops, SparseCore 0:
  205.7 139.1 all-reduce.9
  901.3 733.3 all-reduce.5
  1918.8 733.2 all-reduce.7
where the time goes:
time: 2700 us; the launch traced here: 2690 us
  waiting for transfers between devices  1570 us (58%)
  matrix products  707 us (26%)
  local copies, waits for them, and re-layouts  146 us (5%)
  other arithmetic  135 us (5%)
  blocking collectives  97.4 us (4%)
    psum x1, waiting for transfers between devices, device_layer(): lax.psum(jnp.einsum('rhe,hed->rd', attn_rows, w_out, preferred_element_ty...  733 us
    psum x1, waiting for transfers between devices, device_layer(): lax.psum(jnp.dot(gelu_rows, w_down, preferred_element_type=jnp.float32),...  733 us
    dot_general x1, matrix products, device_layer(): jnp.dot(hidden, w_up, preferred_element_type=jnp.float32)  143 us
    dot_general x1, matrix products, device_layer(): jnp.dot(gelu_rows, w_down, preferred_element_type=jnp.float32)  141 us
    psum x1, waiting for transfers between devices, device_layer(): q_glob, k_glob, v_glob = lax.psum(picked, 'sp')  102 us
    psum x1, blocking collectives, global_queries(): return lax.psum(part_out, 'sp').astype(jnp.bfloat16)  76.4 us
    dot_general x16, matrix products, one_block(): jnp.einsum('hqk,khe->qhe', p_win, v_blk, preferred_element_type=jnp.float32)  64.5 us
  transfers between devices with their start and end apart: 7, of which 3 were waited for; matrix products, arithmetic and copies ran while one was open for 1% of the time, Pallas kernels for 0%

commit v1 on v0

v1 whole, which is shorter than its diff:
```python
import functools
import math

import jax
import jax.numpy as jnp
from jax import lax
from jax.experimental import pallas as pl
from jax.experimental.pallas import tpu as pltpu
from jax.sharding import PartitionSpec as P


WIN = 256
QB = 256
ROWS = 512
F32 = jnp.float32
BF16 = jnp.bfloat16
LOG2E = 1.4426950408889634


def contract_last(a, b):
    return lax.dot_general(a, b, (((1,), (1,)), ((), ())), preferred_element_type=F32)


def contract_first(a, b):
    return lax.dot_general(a, b, (((0,), (0,)), ((), ())), preferred_element_type=F32)


def window_kernel(r0_ref, q_ref, k_ref, v_ref, lk_ref, lv_ref, rk_ref, rv_ref, kg_ref, vg_ref, bias_ref, o_ref,
                  k_win, v_win, mask, *, coef):
    n_rows = k_ref.shape[1]
    r0 = pl.multiple_of(r0_ref[0], ROWS)

    @pl.when(pl.program_id(0) == 0)
    def _():
        key = lax.broadcasted_iota(jnp.int32, (QB + 2 * WIN, QB), 0)
        query = lax.broadcasted_iota(jnp.int32, (QB + 2 * WIN, QB), 1)
        band = (key >= query) & (key <= query + 2 * WIN)
        for b in range(ROWS // QB):
            rows = bias_ref[pl.ds(pl.multiple_of(r0 + b * QB, QB), QB + 2 * WIN), :]
            mask[b] = jnp.where(band, jnp.concatenate([rows] * (QB // 128), axis=1), -jnp.inf)

    before = pl.multiple_of(jnp.maximum(r0 - WIN, 0), WIN)
    after = pl.multiple_of(jnp.minimum(r0 + ROWS, n_rows - WIN), WIN)
    for src, left, right, dst in ((k_ref, lk_ref, rk_ref, k_win), (v_ref, lv_ref, rv_ref, v_win)):
        dst[0:WIN, :] = jnp.where(r0 == 0, left[0], src[0, pl.ds(before, WIN), :])
        dst[WIN:WIN + ROWS, :] = src[0, pl.ds(r0, ROWS), :]
        dst[WIN + ROWS:, :] = jnp.where(r0 + ROWS == n_rows, right[0], src[0, pl.ds(after, WIN), :])

    def scores(b):
        q_blk = q_ref[0, b * QB:(b + 1) * QB, :]
        s_win = contract_last(k_win[b * QB:(b + 1) * QB + 2 * WIN, :], q_blk) * coef + mask[b]
        return s_win, contract_last(kg_ref[0], q_blk) * coef

    s_win, s_glob = scores(0)
    for b in range(ROWS // QB):
        following = scores(b + 1) if b + 1 < ROWS // QB else (None, None)
        top = jnp.maximum(jnp.max(s_win, axis=0, keepdims=True), jnp.max(s_glob, axis=0, keepdims=True))
        e_win = jnp.exp2(s_win - top)
        e_glob = jnp.exp2(s_glob - top)
        inv = 1.0 / (jnp.sum(e_win, axis=0, keepdims=True) + jnp.sum(e_glob, axis=0, keepdims=True))
        out = contract_first(v_win[b * QB:(b + 1) * QB + 2 * WIN, :], (e_win * inv).astype(BF16))
        out = out + contract_first(vg_ref[0], (e_glob * inv).astype(BF16))
        o_ref[b * QB:(b + 1) * QB, :] = out.T.astype(BF16)
        s_win, s_glob = following


def window_rows(r0, q, k, v, left_k, left_v, right_k, right_v, k_glob, v_glob, bias):
    n_heads, n_rows, dim = q.shape
    n_glob = k_glob.shape[1]

    def head(shape):
        return pl.BlockSpec((1,) + shape, lambda h, r: (h, 0, 0))

    span = ROWS + 2 * WIN
    work = n_heads * ROWS * (QB + 2 * WIN + n_glob)
    return pl.pallas_call(
        functools.partial(window_kernel, coef=LOG2E / math.sqrt(dim)),
        out_shape=jax.ShapeDtypeStruct((ROWS, n_heads * dim), BF16),
        grid_spec=pltpu.PrefetchScalarGridSpec(
            num_scalar_prefetch=1,
            grid=(n_heads,),
            in_specs=[
                pl.BlockSpec((1, ROWS, dim), lambda h, r: (h, r[0] // ROWS, 0)),
                head((n_rows, dim)), head((n_rows, dim)),
                head((WIN, dim)), head((WIN, dim)), head((WIN, dim)), head((WIN, dim)),
                head((n_glob, dim)), head((n_glob, dim)),
                pl.BlockSpec(bias.shape, lambda h, r: (0, 0)),
            ],
            out_specs=pl.BlockSpec((ROWS, dim), lambda h, r: (0, h)),
            scratch_shapes=[
                pltpu.VMEM((span, dim), BF16),
                pltpu.VMEM((span, dim), BF16),
                pltpu.VMEM((ROWS // QB, QB + 2 * WIN, QB), F32),
            ],
        ),
        cost_estimate=pl.CostEstimate(flops=8 * work * dim, bytes_accessed=28 << 20, transcendentals=work),
        compiler_params=pltpu.CompilerParams(dimension_semantics=("arbitrary",), vmem_limit_bytes=62 << 20),
        name="window_attention",
    )(r0, q, k, v, left_k, left_v, right_k, right_v, k_glob, v_glob, bias)


def glob_kernel(q_ref, k_ref, v_ref, o_ref, *, coef):
    dim = q_ref.shape[2]
    n_blocks = q_ref.shape[1] // QB

    def scores(b):
        return contract_last(k_ref[0], q_ref[0, b * QB:(b + 1) * QB, :]) * coef

    s = scores(0)
    for b in range(n_blocks):
        following = scores(b + 1) if b + 1 < n_blocks else None
        cols = slice(b * QB, (b + 1) * QB)
        top = jnp.max(s, axis=0, keepdims=True)
        e = jnp.exp2(s - top)
        total = jnp.sum(e, axis=0, keepdims=True)
        o_ref[0, 0:dim, cols] = contract_first(v_ref[0], (e * (1.0 / total)).astype(BF16))
        row = lax.broadcasted_iota(jnp.int32, (8, QB), 0)
        o_ref[0, dim:, cols] = jnp.where(row == 0, top, total)
        s = following


def glob_part(q_glob, k, v):
    n_heads, n_glob, dim = q_glob.shape
    n_rows = k.shape[1]
    work = n_heads * n_rows * n_glob

    def head(shape):
        return pl.BlockSpec((1,) + shape, lambda h: (h, 0, 0))

    return pl.pallas_call(
        functools.partial(glob_kernel, coef=LOG2E / math.sqrt(dim)),
        out_shape=jax.ShapeDtypeStruct((n_heads, dim + 8, n_glob), F32),
        grid=(n_heads,),
        in_specs=[head((n_glob, dim)), head((n_rows, dim)), head((n_rows, dim))],
        out_specs=head((dim + 8, n_glob)),
        cost_estimate=pl.CostEstimate(flops=8 * work * dim, bytes_accessed=24 << 20, transcendentals=work),
        compiler_params=pltpu.CompilerParams(dimension_semantics=("arbitrary",), vmem_limit_bytes=62 << 20),
        name="global_queries",
    )(q_glob, k, v)


def merge_parts(parts, dim):
    tops = [p[:, dim:dim + 1, :] for p in parts]
    top = functools.reduce(jnp.maximum, tops)
    weights = [p[:, dim + 1:dim + 2, :] * jnp.exp2(t - top) for p, t in zip(parts, tops)]
    inv = 1.0 / functools.reduce(jnp.add, weights)
    return functools.reduce(jnp.add, [p[:, :dim, :] * (w * inv) for p, w in zip(parts, weights)]).astype(BF16)


def hidden_kernel(where_ref, gpos_ref, om_ref, oo_ref, gm_ref, go_ref, x_ref, wm_ref, w0_ref, w1_ref, h_ref, mine, other):
    size = x_ref.shape[0]
    n_parts, _, part = other.shape

    @pl.when(pl.program_id(0) == 0)
    def _():
        row = where_ref[1] + lax.broadcasted_iota(jnp.int32, (size, gpos_ref.shape[1]), 0)
        hit = jnp.where(row == gpos_ref[...], 1.0, 0.0)
        is_glob = jnp.max(hit, axis=1, keepdims=True) > 0.0
        pick = hit.astype(BF16)
        for i in range(n_parts):
            cols = slice(i * part, (i + 1) * part)
            rows = contract_last(pick, gm_ref[0, cols, :])
            mine[:, cols] = jnp.where(is_glob, rows, om_ref[:, cols].astype(F32)).astype(BF16)
            rows = contract_last(pick, go_ref[0, cols, :])
            other[i] = jnp.where(is_glob, rows, oo_ref[:, cols].astype(F32)).astype(BF16)

    a_mine = jnp.dot(mine[...], wm_ref[...], preferred_element_type=F32)
    a_other = jnp.dot(other[where_ref[2]], w0_ref[...], preferred_element_type=F32)
    a_other = a_other + jnp.dot(other[where_ref[3]], w1_ref[...], preferred_element_type=F32)
    h_ref[...] = (x_ref[...].astype(F32) + (a_mine + a_other)).astype(BF16)


def hidden_block(where, gpos, o_mine, o_other, glob, x, wo_mine, wo_parts, local, size):
    heads, width = wo_mine.shape
    n_glob = gpos.shape[1]
    tile = 512
    n_parts = len(wo_parts)
    part = heads // n_parts
    return pl.pallas_call(
        hidden_kernel,
        out_shape=jax.ShapeDtypeStruct((size, width), BF16),
        grid_spec=pltpu.PrefetchScalarGridSpec(
            num_scalar_prefetch=1,
            grid=(width // tile,),
            in_specs=[
                pl.BlockSpec((1, n_glob), lambda j, r: (0, 0)),
                pl.BlockSpec((size, heads), lambda j, r: (local, 0)),
                pl.BlockSpec((size, heads), lambda j, r: (local, 0)),
                pl.BlockSpec((1, heads, n_glob), lambda j, r: (0, 0, 0)),
                pl.BlockSpec((1, heads, n_glob), lambda j, r: (1, 0, 0)),
                pl.BlockSpec((size, tile), lambda j, r: (r[0], j)),
                pl.BlockSpec((heads, tile), lambda j, r: (0, j)),
            ] + [pl.BlockSpec((part, tile), lambda j, r: (0, j))] * n_parts,
            out_specs=pl.BlockSpec((size, tile), lambda j, r: (0, j)),
            scratch_shapes=[pltpu.VMEM((size, heads), BF16), pltpu.VMEM((n_parts, size, part), BF16)],
        ),
        cost_estimate=pl.CostEstimate(flops=4 * size * heads * (width + n_glob), bytes_accessed=40 << 20, transcendentals=0),
        compiler_params=pltpu.CompilerParams(dimension_semantics=("arbitrary",), vmem_limit_bytes=62 << 20),
        name="hidden_rows",
    )(where, gpos, o_mine, o_other, glob, glob, x, wo_mine, *wo_parts)


def gate(value, *deps):
    return lax.optimization_barrier((value,) + deps)[0]


def solution(mesh):
    n_seq = mesh.shape['sp']
    to_right = [(i, i + 1) for i in range(n_seq - 1)]
    to_left = [(i + 1, i) for i in range(n_seq - 1)]
    swap = [(0, 1), (1, 0)]
    swap_core = [(i, i ^ 1) for i in range(n_seq)]
    swap_chip = [(i, i ^ 2) for i in range(n_seq)]

    def device_layer(tokens, glob_pos, w_query, w_key, w_value, w_out, w_up, w_down):
        n_rows, width = tokens.shape
        n_heads, dim = w_query.shape[1:]
        n_glob = glob_pos.shape[0]
        seq_len = n_rows * n_seq
        sp, tp = lax.axis_index('sp'), lax.axis_index('tp')
        first_row = sp * n_rows
        heads = n_heads * dim
        half = n_rows // 2
        away, home = (1 - tp) * half, tp * half
        quarters = [sp, sp ^ 2, sp ^ 1, sp ^ 3]

        row_ids = first_row + jnp.arange(n_rows)
        pick = (glob_pos[:, None] == row_ids[None, :]).astype(BF16)
        picked = jnp.dot(pick, tokens, preferred_element_type=F32).astype(BF16)
        chip_sum = picked + lax.ppermute(picked, 'sp', swap_core)
        core = sp % 2
        side = lax.dynamic_slice_in_dim(chip_sum, core * (width // 2), width // 2, axis=1)
        side = side + lax.ppermute(side, 'sp', swap_chip)
        side_other = lax.ppermute(side, 'sp', swap_core)
        x_glob = jnp.where(core == 0, jnp.concatenate([side, side_other], axis=1),
                           jnp.concatenate([side_other, side], axis=1))

        wo_mine = w_out.reshape(heads, width)
        part = heads // 2
        wo_0 = lax.ppermute(lax.dynamic_slice_in_dim(wo_mine, core * part, part), 'tp', swap)
        wo_parts = (wo_0, lax.ppermute(wo_0, 'sp', swap_core))

        key_pos = first_row - WIN + jnp.arange(n_rows + 2 * WIN)
        key_glob = jnp.any(key_pos[:, None] == glob_pos[None, :], axis=1)
        key_ok = (key_pos >= 0) & (key_pos < seq_len) & jnp.logical_not(key_glob)
        bias = jnp.broadcast_to(jnp.where(key_ok, 0.0, -jnp.inf)[:, None], (n_rows + 2 * WIN, 128)).astype(F32)

        def project(rows, weight):
            return jnp.einsum('rd,dhe->hre', rows, weight, preferred_element_type=F32).astype(BF16)

        k_rows = project(gate(tokens, picked, bias), w_key)
        left_k = lax.ppermute(k_rows[:, n_rows - WIN:], 'sp', to_right)
        right_k = lax.ppermute(k_rows[:, :WIN], 'sp', to_left)
        v_rows = project(gate(tokens, k_rows), w_value)
        left_v = lax.ppermute(v_rows[:, n_rows - WIN:], 'sp', to_right)
        right_v = lax.ppermute(v_rows[:, :WIN], 'sp', to_left)
        q_rows = project(gate(tokens, v_rows), w_query)
        x_glob = gate(x_glob, q_rows)

        q_glob = project(x_glob, w_query)
        mine = glob_part(q_glob, k_rows, v_rows)
        share = n_glob // n_seq
        parts = [lax.dynamic_slice_in_dim(mine, sp * share, share, axis=2)]
        for step in range(1, n_seq):
            dest = lax.rem(sp + step, n_seq)
            piece = lax.dynamic_slice_in_dim(mine, dest * share, share, axis=2)
            parts.append(lax.ppermute(piece, 'sp', [(i, (i + step) % n_seq) for i in range(n_seq)]))
        k_glob = project(gate(x_glob, mine), w_key)
        v_glob = project(gate(x_glob, k_glob), w_value)

        def window(start, *deps):
            row = gate(start.reshape(1), *deps)
            return window_rows(row, q_rows, k_rows, v_rows, left_k, left_v, right_k, right_v, k_glob, v_glob, bias)

        att, att_other = {}, {}
        att['h0'] = window(home)
        merged = merge_parts([gate(parts[0], att['h0'])] + parts[1:], dim).reshape(heads, share)
        merged_other = lax.ppermute(merged, 'tp', swap)
        att_other['a0'] = lax.ppermute(gate(att['h0'], merged), 'tp', swap)
        att['h1'] = window(home + ROWS, merged)
        att_other['a1'] = lax.ppermute(att['h1'], 'tp', swap)
        glob = jnp.stack([merged, gate(merged_other, att['h1'])])
        glob = jnp.concatenate([glob, lax.ppermute(glob, 'sp', swap_chip)], axis=2)
        att['a0'] = window(away, att['h1'])
        att_other['h0'] = lax.ppermute(att['a0'], 'tp', swap)
        glob = gate(glob, att['a0'])
        glob = jnp.concatenate([glob, lax.ppermute(glob, 'sp', swap_core)], axis=2)
        gpos = jnp.concatenate([lax.dynamic_slice_in_dim(glob_pos, q * share, share) for q in quarters]).reshape(1, n_glob)

        def hidden_rows(key, start, offset, size, dep):
            row = start + offset
            where = jnp.stack([row // size, first_row + row, core, 1 - core]).astype(jnp.int32)
            return hidden_block(gate(where, dep), gpos, att[key], att_other[key], glob, tokens, wo_mine, wo_parts,
                                (offset % ROWS) // size, size)

        def mlp(h_blk):
            u = jax.nn.gelu(jnp.dot(h_blk, w_up, preferred_element_type=F32), approximate=True).astype(BF16)
            return lax.optimization_barrier(jnp.dot(u, w_down, preferred_element_type=F32))

        sums, dep = [], att['a0']
        for i, (key, offset, size) in enumerate((('a0', 0, 256), ('a0', 256, 256), ('a1', 512, 512))):
            dep = partial = mlp(hidden_rows(key, away, offset, size, dep))
            sums.append(lax.ppermute(partial, 'tp', swap))
            if i == 0:
                dep = att['a1'] = window(away + ROWS, partial)
                att_other['h1'] = lax.ppermute(att['a1'], 'tp', swap)

        def finish(h_blk, partial, total):
            return lax.optimization_barrier((h_blk.astype(F32) + (partial + total)).astype(BF16))

        pieces, y_other = [], []
        for c, arrived in ((0, sums[:2]), (1, sums[2:])):
            h_blk = hidden_rows('h%d' % c, home, c * ROWS, ROWS, dep)
            dep = partial = mlp(h_blk)
            size = ROWS // len(arrived)
            for i, total in enumerate(arrived):
                y = finish(h_blk[i * size:(i + 1) * size], partial[i * size:(i + 1) * size], gate(total, partial))
                y_other.append(lax.ppermute(y, 'tp', swap))
                pieces.append((y, c * ROWS + i * size))
        out = gate(jnp.zeros((n_rows, width), BF16), dep)
        for y, offset in pieces:
            out = lax.dynamic_update_slice_in_dim(out, y, home + offset, 0)
        for y, (_, offset) in zip(y_other, pieces):
            out = lax.dynamic_update_slice_in_dim(gate(out, pieces[-1][0]), y, away + offset, 0)
        return out

    row_spec = P(('dp', 'sp'), None)
    head_spec = P(None, 'tp', None)
    in_specs = (row_spec, P('dp'), head_spec, head_spec, head_spec, P('tp', None, None), P(None, 'tp'), P('tp', None))
    return jax.shard_map(device_layer, mesh=mesh, in_specs=in_specs, out_specs=row_spec, check_vma=False)
```

time: 2700 us -> 1180 us (0.44)
  waiting for transfers between devices: 1570 us -> 259 us
  Pallas kernels: 0 us -> 267 us
  matrix products: 707 us -> 524 us
  local copies, waits for them, and re-layouts: 146 us -> 43.9 us
  blocking collectives: 97.4 us -> 0 us
  other arithmetic: 135 us -> 43.1 us
    psum x3 -> x0, waiting for transfers between devices: 1570 us -> none  [the longest x1 733 us: device_layer(): lax.psum(jnp.einsum('rhe,hed->rd', attn_rows, w_out, preferred_element_ty...]
    pallas_call x0 -> x10, Pallas kernels: none -> 267 us  [the longest x5 130 us: hidden_block(): pl.pallas_call(hidden_kernel, out_shape=jax.ShapeDtypeStruct((size, width...]
    ppermute x4 -> x25, waiting for transfers between devices: 0.01 us -> 259 us  [the longest x3 161 us: device_layer(): y_other.append(lax.ppermute(y, 'tp', swap))]
    dot_general x72 -> x17, matrix products: 707 us -> 524 us  [the longest x5 173 us: mlp(): jnp.dot(h_blk, w_up, preferred_element_type=F32)]
    psum x2 -> x0, blocking collectives: 87 us -> none  [the longest x1 76.4 us: global_queries(): return lax.psum(part_out, 'sp').astype(jnp.bfloat16)]
    reduce_sum x33 -> x0, other arithmetic: 65.1 us -> none  [the longest x16 23 us: one_block(): jnp.sum(e_win, axis=2, keepdims=True)]
    convert_element_type x4 -> x0, local copies, waits for them, and re-layouts: 48.4 us -> none  [the longest x1 24.4 us: device_layer(): jnp.einsum('rd,dhe->rhe', tokens, w_value, preferred_element_type=jnp.flo...]
    scatter x1 -> x0, local copies, waits for them, and re-layouts: 45.7 us -> none  [device_layer(): attn_rows.at[jnp.where(owned, local_idx, n_rows)].set(glob_out, mode='drop')]
  transfers between devices with their start and end apart: 7 -> 25, of which waited for: 3 -> 4; matrix products, arithmetic and copies ran while one was open for 1% -> 49% of each run, Pallas kernels for 0% -> 23%
where the time goes in v1:
time: 1180 us; the launch traced here: 1170 us
  matrix products  524 us (44%)
  Pallas kernels  267 us (23%)
  waiting for transfers between devices  259 us (22%)
  local copies, waits for them, and re-layouts  43.9 us (4%)
  other arithmetic  43.1 us (4%)
  starting transfers between devices  29.4 us (2%)
    dot_general x5, matrix products, mlp(): jnp.dot(h_blk, w_up, preferred_element_type=F32)  173 us
    dot_general x6, matrix products, project(): jnp.einsum('rd,dhe->hre', rows, weight, preferred_element_type=F32)  170 us
    dot_general x5, matrix products, mlp(): jnp.dot(u, w_down, preferred_element_type=F32)  165 us
    ppermute x3, waiting for transfers between devices, device_layer(): y_other.append(lax.ppermute(y, 'tp', swap))  161 us
    pallas_call x5, Pallas kernels, hidden_block(): pl.pallas_call(hidden_kernel, out_shape=jax.ShapeDtypeStruct((size, width...  130 us
    pallas_call x4, Pallas kernels, window_rows(): pl.pallas_call(functools.partial(window_kernel, coef=LOG2E / math.sqrt(di...  102 us
    ppermute x1, waiting for transfers between devices, device_layer(): lax.ppermute(lax.dynamic_slice_in_dim(wo_mine, core * part, part), 'tp',...  58.2 us
    ppermute x1, waiting for transfers between devices, device_layer(): att_other['a0'] = lax.ppermute(gate(att['h0'], merged), 'tp', swap)  39.2 us
  transfers between devices with their start and end apart: 25, of which 4 were waited for; matrix products, arithmetic and copies ran while one was open for 49% of the time, Pallas kernels for 23%

profile of v1, /device:TPU:0, one launch (start us, length us, event | category | flops | bytes accessed | tf_op | source)
XLA Modules:
  0.0 1167.4 jit_solution(2456340891554826205)
XLA Ops:
  0.0 15.7 %convolution_convert_fusion = bf16[512,4096]{1,0:T(8,128)(2,1)} fusion(bf16[2048,4096]{1,0:T(8,128)(2,1)} %x_ref.9, s32[2048]{0:T(1024)S(1)} %iota_add_fusion.1, s32[512]{0:T(512)} %param.9), kind=kOutput, calls=%fused_computation.79 | convolution fusion | flops 8593080320 | bytes 20981760 | tf_op jit(solution)/shard_map/dot_general | solution.py:229
  16.6 1.7 compare_reduce_fusion
  18.3 1.5 broadcast_in_dim.24.bias_ref
  19.8 42.9 %convert_bitcast_fusion.2.k_ref = bf16[16,2048,128]{2,1,0:T(8,128)(2,1)} fusion(bf16[4096,16,128]{2,1,0:T(8,128)(2,1)} %param.11, bf16[2048,4096]{1,0:T(8,128)(2,1)} %x_ref.9), kind=kOutput, calls=%fused_computation.47 | convolution fusion | flops 34363932672 | bytes 41943040 | tf_op jit(solution)/shard_map/rd,dhe->hre/dot_general | solution.py:249
  62.8 3.0 dynamic-slice_add_fusion
  65.8 2.5 collective-permute-start.1
  68.3 42.6 %convert_bitcast_fusion.1.v_ref = bf16[16,2048,128]{2,1,0:T(8,128)(2,1)} fusion(bf16[4096,16,128]{2,1,0:T(8,128)(2,1)} %param.12, bf16[2048,4096]{1,0:T(8,128)(2,1)} %x_ref.9), kind=kOutput, calls=%fused_computation.46 | convolution fusion | flops 34363932672 | bytes 41943040 | tf_op jit(solution)/shard_map/rd,dhe->hre/dot_general | solution.py:249
  110.9 3.1 fusion.144
  114.0 3.1 collective-permute-start.4
  118.4 3.1 fusion.145
  121.5 4.0 collective-permute-start.3
  125.5 7.7 constant_dynamic-slice_fusion
  133.2 1.5 collective-permute-start.14
  134.8 3.7 add.213
  138.5 42.6 %convert_bitcast_fusion.q_ref = bf16[16,2048,128]{2,1,0:T(8,128)(2,1)} fusion(bf16[4096,16,128]{2,1,0:T(8,128)(2,1)} %param.10, bf16[2048,4096]{1,0:T(8,128)(2,1)} %x_ref.9), kind=kOutput, calls=%fused_computation.45 | convolution fusion | flops 34363932672 | bytes 41943040 | tf_op jit(solution)/shard_map/rd,dhe->hre/dot_general | solution.py:249
  182.3 4.0 maximum_select_fusion
  186.4 2.0 copy-done.4
  188.3 13.4 %convert_bitcast_fusion.5.q_ref = bf16[16,512,128]{2,1,0:T(8,128)(2,1)} fusion(bf16[4096,16,128]{2,1,0:T(8,128)(2,1)} %param.10, bf16[512,4096]{1,0:T(8,128)(2,1)S(1)} %maximum_select_fusion), kind=kOutput, calls=%fused_computation.106 | convolution fusion | flops 8590983168 | bytes 23068672 | tf_op jit(solution)/shard_map/rd,dhe->hre/dot_general | solution.py:249
  201.8 34.5 %global_queries.1 = f32[16,136,512]{2,1,0:T(8,128)} custom-call(bf16[16,512,128]{2,1,0:T(8,128)(2,1)} %convert_bitcast_fusion.5.q_ref, bf16[16,2048,128]{2,1,0:T(8,128)(2,1)} %convert_bitcast_fusion.2.k_ref, bf16[16,2048,128]{2,1,0:T(8,128)(2,1)} %convert_bitcast_fusion.1.v_ref), custom_call_target="tpu_custom_call" | custom-call | flops 17179869184 | bytes 25165824 | tf_op jit(solution)/shard_map/global_queries/pallas_call | solution.py:130
  236.2 14.8 %convert_bitcast_fusion.4.kg_ref = bf16[16,512,128]{2,1,0:T(8,128)(2,1)} fusion(bf16[4096,16,128]{2,1,0:T(8,128)(2,1)} %param.11, bf16[512,4096]{1,0:T(8,128)(2,1)} %copy-done.4), kind=kOutput, calls=%fused_computation.105 | convolution fusion | flops 8590983168 | bytes 23068672 | tf_op jit(solution)/shard_map/rd,dhe->hre/dot_general | solution.py:249
  251.0 2.0 constant_dynamic-slice_fusion.4
  254.2 1.7 collective-permute-start.8
  255.8 1.4 collective-permute-start.9
  257.3 58.2 %collective-permute-done.14.w0_ref = bf16[1024,4096]{1,0:T(8,128)(2,1)} collective-permute-done((bf16[1024,4096]{1,0:T(8,128)(2,1)}, bf16[1024,4096]{1,0:T(8,128)(2,1)}, u32[]{:S(2)}, u32[]{:S(2)}) %collective-permute-start.14) | collective-permute-done | bytes 8388640 | tf_op jit(solution)/shard_map/ppermute | solution.py:240
  315.5 13.7 %convert_bitcast_fusion.3.vg_ref = bf16[16,512,128]{2,1,0:T(8,128)(2,1)} fusion(bf16[4096,16,128]{2,1,0:T(8,128)(2,1)} %param.12, bf16[512,4096]{1,0:T(8,128)(2,1)S(1)} %copy-done.5), kind=kOutput, calls=%fused_computation.104 | convolution fusion | flops 8590983168 | bytes 23068672 | tf_op jit(solution)/shard_map/rd,dhe->hre/dot_general | solution.py:249
  329.2 25.6 %window_attention.4.om_ref = bf16[512,2048]{1,0:T(8,128)(2,1)} custom-call(s32[1]{0:T(128)} %bitcast.23.r0_ref, bf16[16,2048,128]{2,1,0:T(8,128)(2,1)} %convert_bitcast_fusion.q_ref, bf16[16,2048,128]{2,1,0:T(8,128)(2,1)} %convert_bitcast_fusion.2.k_ref, bf16[16,2048,128]{2,1,0:T(8,128)(2,1)} %convert_bitcast_fusion.1.v_ref, ...), custom_call_target="tpu_custom_call" | custom-call | flops 10737418240 | bytes 29360128 | tf_op jit(solution)/shard_map/window_attention/pallas_call | solution.py:76
  356.9 2.7 fusion.120
  359.7 1.8 collective-permute-start.11
  361.4 25.6 %window_attention.5.om_ref = bf16[512,2048]{1,0:T(8,128)(2,1)} custom-call(s32[1]{0:T(128)} %bitcast.14.r0_ref, bf16[16,2048,128]{2,1,0:T(8,128)(2,1)} %convert_bitcast_fusion.q_ref, bf16[16,2048,128]{2,1,0:T(8,128)(2,1)} %convert_bitcast_fusion.2.k_ref, bf16[16,2048,128]{2,1,0:T(8,128)(2,1)} %convert_bitcast_fusion.1.v_ref, ...), custom_call_target="tpu_custom_call" | custom-call | flops 10737418240 | bytes 29360128 | tf_op jit(solution)/shard_map/window_attention/pallas_call | solution.py:76
  388.1 25.6 %window_attention.6.om_ref = bf16[512,2048]{1,0:T(8,128)(2,1)} custom-call(s32[1]{0:T(128)} %bitcast.13.r0_ref, bf16[16,2048,128]{2,1,0:T(8,128)(2,1)} %convert_bitcast_fusion.q_ref, bf16[16,2048,128]{2,1,0:T(8,128)(2,1)} %convert_bitcast_fusion.2.k_ref, bf16[16,2048,128]{2,1,0:T(8,128)(2,1)} %convert_bitcast_fusion.1.v_ref, ...), custom_call_target="tpu_custom_call" | custom-call | flops 10737418240 | bytes 29360128 | tf_op jit(solution)/shard_map/window_attention/pallas_call | solution.py:76
  413.8 1.5 pad_maximum_fusion
  418.4 1.7 collective-permute-start.16
  420.4 1.5 constant_dynamic-update-slice_fusion.1
  421.9 3.1 constant_dynamic-update-slice_fusion.gm_ref.go_ref
  425.0 39.2 %collective-permute-done.10.oo_ref = bf16[512,2048]{1,0:T(8,128)(2,1)} collective-permute-done((bf16[512,2048]{1,0:T(8,128)(2,1)}, bf16[512,2048]{1,0:T(8,128)(2,1)}, u32[]{:S(2)}, u32[]{:S(2)}) %collective-permute-start.10) | collective-permute-done | bytes 2097184 | tf_op jit(solution)/shard_map/ppermute | solution.py:279
  464.3 21.6 %hidden_rows.5 = bf16[256,4096]{1,0:T(8,128)(2,1)} custom-call(s32[4]{0:T(128)} %get-tuple-element.39.where_ref, s32[1,512]{1,0:T(1,128)} %bitcast.134, bf16[512,2048]{1,0:T(8,128)(2,1)} %window_attention.6.om_ref, bf16[512,2048]{1,0:T(8,128)(2,1)} %collective-permute-done.10.oo_ref, bf16[2,2048,512]{2,1,0:T(8,128)(2,1)} %constant_dynamic-update-slice_fusion.gm_ref.go_ref, ...), custom_call_target="tpu_custom_call" | custom-call | flops 9663676416 | bytes 41943040 | tf_op jit(solution)/shard_map/hidden_rows/pallas_call | solution.py:179
  485.9 27.4 %fusion.206 = bf16[256,7168]{1,0:T(8,128)(2,1)} fusion(bf16[256,4096]{1,0:T(8,128)(2,1)} %hidden_rows.5, bf16[4096,7168]{1,0:T(8,128)(2,1)} %param.14), kind=kOutput, calls=%fused_computation.55.clone.clone | convolution fusion | flops 15048900608 | bytes 64487424 | tf_op jit(solution)/shard_map/dot_general | solution.py:297
  513.3 25.5 %fusion.95 = f32[256,4096]{1,0:T(8,128)} fusion(bf16[7168,4096]{1,0:T(8,128)(2,1)} %param.15, bf16[256,7168]{1,0:T(8,128)(2,1)} %fusion.206), kind=kOutput, calls=%fused_computation.93 | convolution fusion | flops 15032385536 | bytes 66584576 | tf_op jit(solution)/shard_map/dot_general | solution.py:298
  539.2 25.6 %window_attention.7.om_ref = bf16[512,2048]{1,0:T(8,128)(2,1)} custom-call(s32[1]{0:T(128)} %bitcast.10.r0_ref, bf16[16,2048,128]{2,1,0:T(8,128)(2,1)} %convert_bitcast_fusion.q_ref, bf16[16,2048,128]{2,1,0:T(8,128)(2,1)} %convert_bitcast_fusion.2.k_ref, bf16[16,2048,128]{2,1,0:T(8,128)(2,1)} %convert_bitcast_fusion.1.v_ref, ...), custom_call_target="tpu_custom_call" | custom-call | flops 10737418240 | bytes 29360128 | tf_op jit(solution)/shard_map/window_attention/pallas_call | solution.py:76
  564.8 1.7 collective-permute-start.18
  566.5 21.7 %hidden_rows.6 = bf16[256,4096]{1,0:T(8,128)(2,1)} custom-call(s32[4]{0:T(128)} %get-tuple-element.44.where_ref, s32[1,512]{1,0:T(1,128)} %bitcast.135, bf16[512,2048]{1,0:T(8,128)(2,1)} %window_attention.6.om_ref, bf16[512,2048]{1,0:T(8,128)(2,1)} %collective-permute-done.10.oo_ref, bf16[2,2048,512]{2,1,0:T(8,128)(2,1)} %constant_dynamic-update-slice_fusion.gm_ref.go_ref, ...), custom_call_target="tpu_custom_call" | custom-call | flops 9663676416 | bytes 41943040 | tf_op jit(solution)/shard_map/hidden_rows/pallas_call | solution.py:179
  588.1 27.0 %fusion.202 = bf16[256,7168]{1,0:T(8,128)(2,1)} fusion(bf16[256,4096]{1,0:T(8,128)(2,1)} %hidden_rows.6, bf16[4096,7168]{1,0:T(8,128)(2,1)} %param.14), kind=kOutput, calls=%fused_computation.63.clone.clone.1 | convolution fusion | flops 15048900608 | bytes 64487424 | tf_op jit(solution)/shard_map/dot_general | solution.py:297
  615.2 25.5 %fusion.93 = f32[256,4096]{1,0:T(8,128)} fusion(bf16[7168,4096]{1,0:T(8,128)(2,1)} %param.15, bf16[256,7168]{1,0:T(8,128)(2,1)} %fusion.202), kind=kOutput, calls=%fused_computation.92 | convolution fusion | flops 15032385536 | bytes 66584576 | tf_op jit(solution)/shard_map/dot_general | solution.py:298
  641.0 28.8 %hidden_rows.7 = bf16[512,4096]{1,0:T(8,128)(2,1)} custom-call(s32[4]{0:T(128)} %add_add_fusion.2.where_ref, s32[1,512]{1,0:T(1,128)} %bitcast.136, bf16[512,2048]{1,0:T(8,128)(2,1)} %window_attention.7.om_ref, bf16[512,2048]{1,0:T(8,128)(2,1)} %collective-permute-done.16.oo_ref, bf16[2,2048,512]{2,1,0:T(8,128)(2,1)} %constant_dynamic-update-slice_fusion.gm_ref.go_ref, ...), custom_call_target="tpu_custom_call" | custom-call | flops 19327352832 | bytes 41943040 | tf_op jit(solution)/shard_map/hidden_rows/pallas_call | solution.py:179
  669.8 39.5 %fusion.198 = bf16[512,7168]{1,0:T(8,128)(2,1)S(1)} fusion(bf16[512,4096]{1,0:T(8,128)(2,1)} %hidden_rows.7, bf16[4096,7168]{1,0:T(8,128)(2,1)} %param.14), kind=kOutput, calls=%fused_computation.25.clone.clone | convolution fusion | flops 30097801216 | bytes 70254592 | tf_op jit(solution)/shard_map/dot_general | solution.py:297
  709.3 38.0 %fusion.59 = f32[512,4096]{1,0:T(8,128)} fusion(bf16[7168,4096]{1,0:T(8,128)(2,1)} %param.15, bf16[512,7168]{1,0:T(8,128)(2,1)S(1)} %fusion.198), kind=kOutput, calls=%fused_computation.66 | convolution fusion | flops 30064771072 | bytes 74448896 | tf_op jit(solution)/shard_map/dot_general | solution.py:298
  747.3 1.7 collective-permute-start.21
  749.0 29.3 %hidden_rows.8 = bf16[512,4096]{1,0:T(8,128)(2,1)} custom-call(s32[4]{0:T(128)} %get-tuple-element.46.where_ref, s32[1,512]{1,0:T(1,128)} %bitcast.137, bf16[512,2048]{1,0:T(8,128)(2,1)} %window_attention.4.om_ref, bf16[512,2048]{1,0:T(8,128)(2,1)} %collective-permute-done.17.oo_ref, bf16[2,2048,512]{2,1,0:T(8,128)(2,1)} %constant_dynamic-update-slice_fusion.gm_ref.go_ref, ...), custom_call_target="tpu_custom_call" | custom-call | flops 19327352832 | bytes 41943040 | tf_op jit(solution)/shard_map/hidden_rows/pallas_call | solution.py:179
  778.3 39.3 %fusion.194 = bf16[512,7168]{1,0:T(8,128)(2,1)S(1)} fusion(bf16[512,4096]{1,0:T(8,128)(2,1)} %hidden_rows.8, bf16[4096,7168]{1,0:T(8,128)(2,1)} %param.14), kind=kOutput, calls=%fused_computation.33.clone.clone | convolution fusion | flops 30097801216 | bytes 70254592 | tf_op jit(solution)/shard_map/dot_general | solution.py:297
  817.6 38.1 %fusion.57 = f32[512,4096]{1,0:T(8,128)} fusion(bf16[7168,4096]{1,0:T(8,128)(2,1)} %param.15, bf16[512,7168]{1,0:T(8,128)(2,1)S(1)} %fusion.194), kind=kOutput, calls=%fused_computation.65 | convolution fusion | flops 30064771072 | bytes 74448896 | tf_op jit(solution)/shard_map/dot_general | solution.py:298
  855.7 28.9 %hidden_rows.9 = bf16[512,4096]{1,0:T(8,128)(2,1)} custom-call(s32[4]{0:T(128)} %get-tuple-element.47.where_ref, s32[1,512]{1,0:T(1,128)} %bitcast.138, bf16[512,2048]{1,0:T(8,128)(2,1)} %window_attention.5.om_ref, bf16[512,2048]{1,0:T(8,128)(2,1)} %collective-permute-done.18.oo_ref, bf16[2,2048,512]{2,1,0:T(8,128)(2,1)} %constant_dynamic-update-slice_fusion.gm_ref.go_ref, ...), custom_call_target="tpu_custom_call" | custom-call | flops 19327352832 | bytes 41943040 | tf_op jit(solution)/shard_map/hidden_rows/pallas_call | solution.py:179
  884.7 39.5 %fusion.190 = bf16[512,7168]{1,0:T(8,128)(2,1)S(1)} fusion(bf16[512,4096]{1,0:T(8,128)(2,1)} %hidden_rows.9, bf16[4096,7168]{1,0:T(8,128)(2,1)} %param.14), kind=kOutput, calls=%fused_computation.41.clone.clone.1 | convolution fusion | flops 30097801216 | bytes 70254592 | tf_op jit(solution)/shard_map/dot_general | solution.py:297
  924.2 38.3 %fusion.55 = f32[512,4096]{1,0:T(8,128)} fusion(bf16[7168,4096]{1,0:T(8,128)(2,1)} %param.15, bf16[512,7168]{1,0:T(8,128)(2,1)S(1)} %fusion.190), kind=kOutput, calls=%fused_computation.64 | convolution fusion | flops 30064771072 | bytes 74448896 | tf_op jit(solution)/shard_map/dot_general | solution.py:298
  962.5 11.3 add_convert_fusion
  974.1 9.4 fusion.86
  983.5 1.7 collective-permute-start.22
  985.6 1.9 broadcast_in_dim.12
  987.5 2.0 constant_dynamic-update-slice_fusion.7
  990.9 121.7 %collective-permute-done.22 = bf16[256,4096]{1,0:T(8,128)(2,1)} collective-permute-done((bf16[256,4096]{1,0:T(8,128)(2,1)}, bf16[256,4096]{1,0:T(8,128)(2,1)}, u32[]{:S(2)}, u32[]{:S(2)}) %collective-permute-start.22) | collective-permute-done | bytes 2097184 | tf_op jit(solution)/shard_map/ppermute | solution.py:318
  1112.5 1.8 constant_dynamic-update-slice_fusion.4
  1114.4 39.8 %collective-permute-done.23 = bf16[256,4096]{1,0:T(8,128)(2,1)} collective-permute-done((bf16[256,4096]{1,0:T(8,128)(2,1)S(1)}, bf16[256,4096]{1,0:T(8,128)(2,1)}, u32[]{:S(2)}, u32[]{:S(2)}) %collective-permute-start.23) | collective-permute-done | bytes 2097184 | tf_op jit(solution)/shard_map/ppermute | solution.py:318
  1154.2 1.8 constant_dynamic-update-slice_fusion.3
  1156.1 6.1 copy-done
  1162.2 4.7 constant_dynamic-update-slice_fusion.2
  (63 shorter events, 13.9 us)
Async XLA Ops:
  0.0 16.6 %copy-start.6 = (s32[512]{0:T(512)S(1)}, s32[512]{0:T(512)}, u32[]{:S(2)}) copy-start(s32[512]{0:T(512)} %param.9) | copy-start | bytes 6148
  15.7 47.0 %collective-permute-start = (bf16[512,4096]{1,0:T(8,128)(2,1)}, bf16[512,4096]{1,0:T(8,128)(2,1)}, u32[]{:S(2)}, u32[]{:S(2)}) collective-permute-start(bf16[512,4096]{1,0:T(8,128)(2,1)} %convolution_convert_fusion), channel_id=1, source_target_pairs={{0,1},{1,0},{2,3},{3,2},{4,5},{5,4},{6,7},{7,6}} | collective-permute-start | bytes 12582920 | tf_op jit(solution)/shard_map/ppermute | solution.py:230
  65.8 69.0 %collective-permute-start.1 = (bf16[512,2048]{1,0:T(8,128)(2,1)S(1)}, bf16[512,2048]{1,0:T(8,128)(2,1)}, u32[]{:S(2)}, u32[]{:S(2)}) collective-permute-start(bf16[512,2048]{1,0:T(8,128)(2,1)S(1)} %dynamic-slice_add_fusion), channel_id=1, source_target_pairs={{0,2},{1,3},{2,0},{3,1},{4,6},{5,7},{6,4},{7,5}} | collective-permute-start | bytes 6291464 | tf_op jit(solution)/shard_map/ppermute | solution.py:233
  114.0 139.0 %collective-permute-start.4 = (bf16[16,256,128]{2,1,0:T(8,128)(2,1)}, bf16[16,256,128]{2,1,0:T(8,128)(2,1)}, u32[]{:S(2)}, u32[]{:S(2)}) collective-permute-start(bf16[16,256,128]{2,1,0:T(8,128)(2,1)} %get-tuple-element.65), channel_id=1, source_target_pairs={{0,1},{1,2},{2,3},{4,5},{5,6},{6,7}} | collective-permute-start | bytes 3145736 | tf_op jit(solution)/shard_map/ppermute | solution.py:255
  117.1 137.1 %collective-permute-start.6 = (bf16[16,256,128]{2,1,0:T(8,128)(2,1)}, bf16[16,256,128]{2,1,0:T(8,128)(2,1)}, u32[]{:S(2)}, u32[]{:S(2)}) collective-permute-start(bf16[16,256,128]{2,1,0:T(8,128)(2,1)} %get-tuple-element.64), channel_id=1, source_target_pairs={{1,0},{2,1},{3,2},{5,4},{6,5},{7,6}} | collective-permute-start | bytes 3145736 | tf_op jit(solution)/shard_map/ppermute | solution.py:256
  121.5 134.3 %collective-permute-start.3 = (bf16[16,256,128]{2,1,0:T(8,128)(2,1)}, bf16[16,256,128]{2,1,0:T(8,128)(2,1)}, u32[]{:S(2)}, u32[]{:S(2)}) collective-permute-start(bf16[16,256,128]{2,1,0:T(8,128)(2,1)} %get-tuple-element.67), channel_id=1, source_target_pairs={{0,1},{1,2},{2,3},{4,5},{5,6},{6,7}} | collective-permute-start | bytes 3145736 | tf_op jit(solution)/shard_map/ppermute | solution.py:252
  133.2 182.2 %collective-permute-start.14 = (bf16[1024,4096]{1,0:T(8,128)(2,1)}, bf16[1024,4096]{1,0:T(8,128)(2,1)}, u32[]{:S(2)}, u32[]{:S(2)}) collective-permute-start(bf16[1024,4096]{1,0:T(8,128)(2,1)} %constant_dynamic-slice_fusion), channel_id=1, source_target_pairs={{0,4},{4,0},{1,5},{5,1},{2,6},{6,2},{3,7},{7,3}} | collective-permute-start | bytes 25165832 | tf_op jit(solution)/shard_map/ppermute | solution.py:240
  138.5 42.6 %collective-permute-start.2 = (bf16[512,2048]{1,0:T(8,128)(2,1)}, bf16[512,2048]{1,0:T(8,128)(2,1)S(1)}, u32[]{:S(2)}, u32[]{:S(2)}) collective-permute-start(bf16[512,2048]{1,0:T(8,128)(2,1)} %add.213), channel_id=1, source_target_pairs={{0,1},{1,0},{2,3},{3,2},{4,5},{5,4},{6,7},{7,6}} | collective-permute-start | bytes 6291464 | tf_op jit(solution)/shard_map/ppermute | solution.py:234
  181.0 148.2 %collective-permute-start.5 = (bf16[16,256,128]{2,1,0:T(8,128)(2,1)}, bf16[16,256,128]{2,1,0:T(8,128)(2,1)}, u32[]{:S(2)}, u32[]{:S(2)}) collective-permute-start(bf16[16,256,128]{2,1,0:T(8,128)(2,1)} %get-tuple-element.66), channel_id=1, source_target_pairs={{1,0},{2,1},{3,2},{5,4},{6,5},{7,6}} | collective-permute-start | bytes 3145736 | tf_op jit(solution)/shard_map/ppermute | solution.py:253
  186.3 2.0 copy-start.4
  236.2 14.8 %copy-start.2 = (f32[16,136,512]{2,1,0:T(8,128)S(1)}, f32[16,136,512]{2,1,0:T(8,128)}, u32[]{:S(2)}) copy-start(f32[16,136,512]{2,1,0:T(8,128)} %global_queries.1) | copy-start | bytes 13369348
  251.0 64.4 %copy-start.5 = (bf16[512,4096]{1,0:T(8,128)(2,1)S(1)}, bf16[512,4096]{1,0:T(8,128)(2,1)}, u32[]{:S(2)}) copy-start(bf16[512,4096]{1,0:T(8,128)(2,1)} %copy-done.4) | copy-start | bytes 12582916
  253.0 101.8 %copy-start.3 = (f32[16,136,128]{2,1,0:T(8,128)}, f32[16,136,128]{2,1,0:T(8,128)S(1)}, u32[]{:S(2)}) copy-start(f32[16,136,128]{2,1,0:T(8,128)S(1)} %get-tuple-element.36) | copy-start | bytes 3342340
  253.0 101.8 %collective-permute-start.7 = (f32[16,136,128]{2,1,0:T(8,128)}, f32[16,136,128]{2,1,0:T(8,128)}, u32[]{:S(2)}, u32[]{:S(2)}) collective-permute-start(f32[16,136,128]{2,1,0:T(8,128)} %get-tuple-element.71), channel_id=1, source_target_pairs={{0,1},{1,2},{2,3},{3,0},{4,5},{5,6},{6,7},{7,4}} | collective-permute-start | bytes 3342344 | tf_op jit(solution)/shard_map/ppermute | solution.py:267
  254.2 100.7 %collective-permute-start.8 = (f32[16,136,128]{2,1,0:T(8,128)}, f32[16,136,128]{2,1,0:T(8,128)}, u32[]{:S(2)}, u32[]{:S(2)}) collective-permute-start(f32[16,136,128]{2,1,0:T(8,128)} %get-tuple-element.70), channel_id=1, source_target_pairs={{0,2},{1,3},{2,0},{3,1},{4,6},{5,7},{6,4},{7,5}} | collective-permute-start | bytes 3342344 | tf_op jit(solution)/shard_map/ppermute | solution.py:267
  255.8 99.0 %collective-permute-start.9 = (f32[16,136,128]{2,1,0:T(8,128)}, f32[16,136,128]{2,1,0:T(8,128)}, u32[]{:S(2)}, u32[]{:S(2)}) collective-permute-start(f32[16,136,128]{2,1,0:T(8,128)} %get-tuple-element.69), channel_id=1, source_target_pairs={{0,3},{1,0},{2,1},{3,2},{4,7},{5,4},{6,5},{7,6}} | collective-permute-start | bytes 3342344 | tf_op jit(solution)/shard_map/ppermute | solution.py:267
  315.5 148.8 %collective-permute-start.15 = (bf16[1024,4096]{1,0:T(8,128)(2,1)}, bf16[1024,4096]{1,0:T(8,128)(2,1)}, u32[]{:S(2)}, u32[]{:S(2)}) collective-permute-start(bf16[1024,4096]{1,0:T(8,128)(2,1)} %collective-permute-done.14.w0_ref), channel_id=1, source_target_pairs={{0,1},{1,0},{2,3},{3,2},{4,5},{5,4},{6,7},{7,6}} | collective-permute-start | bytes 25165832 | tf_op jit(solution)/shard_map/ppermute | solution.py:241
  359.7 27.4 %collective-permute-start.11 = (bf16[2048,128]{1,0:T(8,128)(2,1)S(1)}, bf16[2048,128]{1,0:T(8,128)(2,1)S(1)}, u32[]{:S(2)}, u32[]{:S(2)}) collective-permute-start(bf16[2048,128]{1,0:T(8,128)(2,1)S(1)} %bitcast.121), channel_id=1, source_target_pairs={{0,4},{4,0},{1,5},{5,1},{2,6},{6,2},{3,7},{7,3}} | collective-permute-start | bytes 1572872 | tf_op jit(solution)/shard_map/ppermute | solution.py:278
  388.1 25.6 %collective-permute-start.12 = (bf16[2,2048,128]{2,1,0:T(8,128)(2,1)}, bf16[2,2048,128]{2,1,0:T(8,128)(2,1)}, u32[]{:S(2)}, u32[]{:S(2)}) collective-permute-start(bf16[2,2048,128]{2,1,0:T(8,128)(2,1)} %pad_maximum_fusion.1), channel_id=1, source_target_pairs={{0,2},{1,3},{2,0},{3,1},{4,6},{5,7},{6,4},{7,5}} | collective-permute-start | bytes 3145736 | tf_op jit(solution)/shard_map/ppermute | solution.py:283
  388.1 29.6 %copy-start.7 = (s32[512]{0:T(512)S(1)}, s32[512]{0:T(512)}, u32[]{:S(2)}) copy-start(s32[512]{0:T(512)} %param.9) | copy-start | bytes 6148
  415.2 6.7 collective-permute-start.13
  415.4 48.8 %collective-permute-start.10 = (bf16[512,2048]{1,0:T(8,128)(2,1)}, bf16[512,2048]{1,0:T(8,128)(2,1)}, u32[]{:S(2)}, u32[]{:S(2)}) collective-permute-start(bf16[512,2048]{1,0:T(8,128)(2,1)} %window_attention.4.om_ref), channel_id=1, source_target_pairs={{0,4},{4,0},{1,5},{5,1},{2,6},{6,2},{3,7},{7,3}} | collective-permute-start | bytes 6291464 | tf_op jit(solution)/shard_map/ppermute | solution.py:279
  418.4 222.6 %collective-permute-start.16 = (bf16[512,2048]{1,0:T(8,128)(2,1)}, bf16[512,2048]{1,0:T(8,128)(2,1)}, u32[]{:S(2)}, u32[]{:S(2)}) collective-permute-start(bf16[512,2048]{1,0:T(8,128)(2,1)} %window_attention.5.om_ref), channel_id=1, source_target_pairs={{0,4},{4,0},{1,5},{5,1},{2,6},{6,2},{3,7},{7,3}} | collective-permute-start | bytes 6291464 | tf_op jit(solution)/shard_map/ppermute | solution.py:281
  420.1 328.9 %collective-permute-start.17 = (bf16[512,2048]{1,0:T(8,128)(2,1)}, bf16[512,2048]{1,0:T(8,128)(2,1)}, u32[]{:S(2)}, u32[]{:S(2)}) collective-permute-start(bf16[512,2048]{1,0:T(8,128)(2,1)} %window_attention.6.om_ref), channel_id=1, source_target_pairs={{0,4},{4,0},{1,5},{5,1},{2,6},{6,2},{3,7},{7,3}} | collective-permute-start | bytes 6291464 | tf_op jit(solution)/shard_map/ppermute | solution.py:285
  538.8 423.6 %collective-permute-start.19 = (f32[256,4096]{1,0:T(8,128)}, f32[256,4096]{1,0:T(8,128)}, u32[]{:S(2)}, u32[]{:S(2)}) collective-permute-start(f32[256,4096]{1,0:T(8,128)} %fusion.95), channel_id=1, source_target_pairs={{0,4},{4,0},{1,5},{5,1},{2,6},{6,2},{3,7},{7,3}} | collective-permute-start | bytes 12582920 | tf_op jit(solution)/shard_map/ppermute | solution.py:303
  564.8 291.0 %collective-permute-start.18 = (bf16[512,2048]{1,0:T(8,128)(2,1)}, bf16[512,2048]{1,0:T(8,128)(2,1)}, u32[]{:S(2)}, u32[]{:S(2)}) collective-permute-start(bf16[512,2048]{1,0:T(8,128)(2,1)} %window_attention.7.om_ref), channel_id=1, source_target_pairs={{0,4},{4,0},{1,5},{5,1},{2,6},{6,2},{3,7},{7,3}} | collective-permute-start | bytes 6291464 | tf_op jit(solution)/shard_map/ppermute | solution.py:306
  640.7 321.8 %collective-permute-start.20 = (f32[256,4096]{1,0:T(8,128)}, f32[256,4096]{1,0:T(8,128)}, u32[]{:S(2)}, u32[]{:S(2)}) collective-permute-start(f32[256,4096]{1,0:T(8,128)} %fusion.93), channel_id=1, source_target_pairs={{0,4},{4,0},{1,5},{5,1},{2,6},{6,2},{3,7},{7,3}} | collective-permute-start | bytes 12582920 | tf_op jit(solution)/shard_map/ppermute | solution.py:303
  747.3 215.2 %collective-permute-start.21 = (f32[512,4096]{1,0:T(8,128)}, f32[512,4096]{1,0:T(8,128)}, u32[]{:S(2)}, u32[]{:S(2)}) collective-permute-start(f32[512,4096]{1,0:T(8,128)} %fusion.59), channel_id=1, source_target_pairs={{0,4},{4,0},{1,5},{5,1},{2,6},{6,2},{3,7},{7,3}} | collective-permute-start | bytes 25165832 | tf_op jit(solution)/shard_map/ppermute | solution.py:303
  973.8 182.3 %collective-permute-start.24 = (bf16[512,4096]{1,0:T(8,128)(2,1)}, bf16[512,4096]{1,0:T(8,128)(2,1)}, u32[]{:S(2)}, u32[]{:S(2)}) collective-permute-start(bf16[512,4096]{1,0:T(8,128)(2,1)} %add_convert_fusion), channel_id=1, source_target_pairs={{0,4},{4,0},{1,5},{5,1},{2,6},{6,2},{3,7},{7,3}} | collective-permute-start | bytes 12582920 | tf_op jit(solution)/shard_map/ppermute | solution.py:318
  983.5 129.0 %collective-permute-start.22 = (bf16[256,4096]{1,0:T(8,128)(2,1)}, bf16[256,4096]{1,0:T(8,128)(2,1)}, u32[]{:S(2)}, u32[]{:S(2)}) collective-permute-start(bf16[256,4096]{1,0:T(8,128)(2,1)} %get-tuple-element.63), channel_id=1, source_target_pairs={{0,4},{4,0},{1,5},{5,1},{2,6},{6,2},{3,7},{7,3}} | collective-permute-start | bytes 6291464 | tf_op jit(solution)/shard_map/ppermute | solution.py:318
  985.2 169.0 %collective-permute-start.23 = (bf16[256,4096]{1,0:T(8,128)(2,1)S(1)}, bf16[256,4096]{1,0:T(8,128)(2,1)}, u32[]{:S(2)}, u32[]{:S(2)}) collective-permute-start(bf16[256,4096]{1,0:T(8,128)(2,1)S(1)} %get-tuple-element.62), channel_id=1, source_target_pairs={{0,4},{4,0},{1,5},{5,1},{2,6},{6,2},{3,7},{7,3}} | collective-permute-start | bytes 6291464 | tf_op jit(solution)/shard_map/ppermute | solution.py:318
  987.5 2.8 copy-start.1
  1156.1 6.2 copy-start

commit v2 on v1

v2 whole, which is shorter than its diff:
```python
import functools
import math

import jax
import jax.numpy as jnp
from jax import lax
from jax.experimental import pallas as pl
from jax.experimental.pallas import tpu as pltpu
from jax.sharding import PartitionSpec as P


WIN = 256
QB = 256
STEP_HEADS = 4
MLP_TILE = 1024
ROWS = 512
F32 = jnp.float32
BF16 = jnp.bfloat16
LOG2E = 1.4426950408889634


def contract_last(a, b):
    return lax.dot_general(a, b, (((1,), (1,)), ((), ())), preferred_element_type=F32)


def contract_first(a, b):
    return lax.dot_general(a, b, (((0,), (0,)), ((), ())), preferred_element_type=F32)


def window_kernel(r0_ref, q_ref, k_ref, v_ref, lk_ref, lv_ref, rk_ref, rv_ref, *refs, coef):
    *globs, bias_ref, o_ref, k_win, v_win, k_all, v_all, mask = refs
    n_globs = len(globs) // 2
    n_rows = k_ref.shape[1]
    r0 = pl.multiple_of(r0_ref[0], ROWS)

    @pl.when(pl.program_id(0) == 0)
    def _():
        key = lax.broadcasted_iota(jnp.int32, (QB + 2 * WIN, QB), 0)
        query = lax.broadcasted_iota(jnp.int32, (QB + 2 * WIN, QB), 1)
        band = (key >= query) & (key <= query + 2 * WIN)
        for b in range(ROWS // QB):
            rows = bias_ref[pl.ds(pl.multiple_of(r0 + b * QB, QB), QB + 2 * WIN), :]
            mask[b] = jnp.where(band, jnp.concatenate([rows] * (QB // 128), axis=1), -jnp.inf)

    before = pl.multiple_of(jnp.maximum(r0 - WIN, 0), WIN)
    after = pl.multiple_of(jnp.minimum(r0 + ROWS, n_rows - WIN), WIN)
    n_heads = k_ref.shape[0]
    for h in range(n_heads):
        for src, left, right, dst in ((k_ref, lk_ref, rk_ref, k_win), (v_ref, lv_ref, rv_ref, v_win)):
            dst[h, 0:WIN, :] = jnp.where(r0 == 0, left[0, h], src[h, pl.ds(before, WIN), :])
            dst[h, WIN:WIN + ROWS, :] = src[h, pl.ds(r0, ROWS), :]
            dst[h, WIN + ROWS:, :] = jnp.where(r0 + ROWS == n_rows, right[0, h], src[h, pl.ds(after, WIN), :])
        for dst, parts in ((k_all, globs[:n_globs]), (v_all, globs[n_globs:])):
            for i, part in enumerate(parts):
                size = part.shape[2]
                dst[h, i * size:(i + 1) * size, :] = part[0, h]

    def scores(h, b):
        q_blk = q_ref[h, b * QB:(b + 1) * QB, :]
        s_win = contract_last(k_win[h, b * QB:(b + 1) * QB + 2 * WIN, :], q_blk) * coef + mask[b]
        return s_win, contract_last(k_all[h], q_blk) * coef

    blocks = [(h, b) for h in range(n_heads) for b in range(ROWS // QB)]
    dim = k_ref.shape[2]
    s_win, s_glob = scores(*blocks[0])
    for i, (h, b) in enumerate(blocks):
        following = scores(*blocks[i + 1]) if i + 1 < len(blocks) else (None, None)
        top = jnp.maximum(jnp.max(s_win, axis=0, keepdims=True), jnp.max(s_glob, axis=0, keepdims=True))
        e_win = jnp.exp2(s_win - top)
        e_glob = jnp.exp2(s_glob - top)
        inv = 1.0 / (jnp.sum(e_win, axis=0, keepdims=True) + jnp.sum(e_glob, axis=0, keepdims=True))
        out = contract_first(v_win[h, b * QB:(b + 1) * QB + 2 * WIN, :], (e_win * inv).astype(BF16))
        out = out + contract_first(v_all[h], (e_glob * inv).astype(BF16))
        o_ref[b * QB:(b + 1) * QB, h * dim:(h + 1) * dim] = out.T.astype(BF16)
        s_win, s_glob = following


def window_rows(r0, q, q_block, k, v, left, right, globs, bias):
    n_heads, n_rows, dim = k.shape
    share = globs[0].shape[2]
    n_glob = share * len(globs)

    def head(shape):
        return pl.BlockSpec((STEP_HEADS,) + shape, lambda h, r: (h, 0, 0))

    def item(i, size):
        return pl.BlockSpec((1, STEP_HEADS, size, dim), lambda h, r: (i, h, 0, 0))

    span = ROWS + 2 * WIN
    work = n_heads * ROWS * (QB + 2 * WIN + n_glob)
    return pl.pallas_call(
        functools.partial(window_kernel, coef=LOG2E / math.sqrt(dim)),
        out_shape=jax.ShapeDtypeStruct((ROWS, n_heads * dim), BF16),
        grid_spec=pltpu.PrefetchScalarGridSpec(
            num_scalar_prefetch=1,
            grid=(n_heads // STEP_HEADS,),
            in_specs=[
                pl.BlockSpec((STEP_HEADS, ROWS, dim), lambda h, r: (h, q_block, 0)),
                head((n_rows, dim)), head((n_rows, dim)),
                item(0, WIN), item(1, WIN), item(0, WIN), item(1, WIN),
                *[item(0, share) for _ in globs], *[item(1, share) for _ in globs],
                pl.BlockSpec(bias.shape, lambda h, r: (0, 0)),
            ],
            out_specs=pl.BlockSpec((ROWS, STEP_HEADS * dim), lambda h, r: (0, h)),
            scratch_shapes=[
                pltpu.VMEM((STEP_HEADS, span, dim), BF16),
                pltpu.VMEM((STEP_HEADS, span, dim), BF16),
                pltpu.VMEM((STEP_HEADS, n_glob, dim), BF16),
                pltpu.VMEM((STEP_HEADS, n_glob, dim), BF16),
                pltpu.VMEM((ROWS // QB, QB + 2 * WIN, QB), F32),
            ],
        ),
        cost_estimate=pl.CostEstimate(flops=8 * work * dim, bytes_accessed=28 << 20, transcendentals=work),
        compiler_params=pltpu.CompilerParams(dimension_semantics=("arbitrary",), vmem_limit_bytes=62 << 20),
        name="window_attention",
    )(r0, q, k, v, left, left, right, right, *globs, *globs, bias)


def glob_kernel(*refs, coef):
    n = (len(refs) - 2) // 2
    q_refs, (k_ref, v_ref), o_refs = refs[:n], refs[n:n + 2], refs[n + 2:]
    share, dim = q_refs[0].shape[2:]
    pair = QB // share

    def scores(h, b):
        q_blk = jnp.concatenate([q[0, h] for q in q_refs[b * pair:(b + 1) * pair]], axis=0)
        return contract_last(k_ref[h], q_blk) * coef

    blocks = [(h, b) for h in range(k_ref.shape[0]) for b in range(n // pair)]
    s = scores(*blocks[0])
    for j, (h, b) in enumerate(blocks):
        following = scores(*blocks[j + 1]) if j + 1 < len(blocks) else None
        top = jnp.max(s, axis=0, keepdims=True)
        e = jnp.exp2(s - top)
        total = jnp.sum(e, axis=0, keepdims=True)
        out = contract_first(v_ref[h], (e * (1.0 / total)).astype(BF16))
        row = lax.broadcasted_iota(jnp.int32, (8, QB), 0)
        stats = jnp.where(row == 0, top, total)
        for i in range(pair):
            o_refs[b * pair + i][h, 0:dim, :] = out[:, i * share:(i + 1) * share]
            o_refs[b * pair + i][h, dim:, :] = stats[:, i * share:(i + 1) * share]
        s = following


def glob_part(globs, k, v):
    n_heads, n_rows, dim = k.shape
    share = globs[0].shape[2]
    work = n_heads * n_rows * share * len(globs)

    def head(shape):
        return pl.BlockSpec((STEP_HEADS,) + shape, lambda h: (h, 0, 0))

    return pl.pallas_call(
        functools.partial(glob_kernel, coef=LOG2E / math.sqrt(dim)),
        out_shape=[jax.ShapeDtypeStruct((n_heads, dim + 8, share), F32)] * len(globs),
        grid=(n_heads // STEP_HEADS,),
        in_specs=[pl.BlockSpec((1, STEP_HEADS, share, dim), lambda h: (2, h, 0, 0))] * len(globs) + [head((n_rows, dim))] * 2,
        out_specs=[head((dim + 8, share))] * len(globs),
        cost_estimate=pl.CostEstimate(flops=8 * work * dim, bytes_accessed=24 << 20, transcendentals=work),
        compiler_params=pltpu.CompilerParams(dimension_semantics=("arbitrary",), vmem_limit_bytes=62 << 20),
        name="global_queries",
    )(*globs, k, v)


def merge_parts(parts, dim):
    tops = [p[:, dim:dim + 1, :] for p in parts]
    top = functools.reduce(jnp.maximum, tops)
    weights = [p[:, dim + 1:dim + 2, :] * jnp.exp2(t - top) for p, t in zip(parts, tops)]
    inv = 1.0 / functools.reduce(jnp.add, weights)
    return functools.reduce(jnp.add, [p[:, :dim, :] * (w * inv) for p, w in zip(parts, weights)]).astype(BF16)


def hidden_kernel(where_ref, gpos_ref, om_ref, oo_ref, *refs):
    *globs, x_ref, wm_ref, w0_ref, w1_ref, h_ref, mine, other = refs
    size = x_ref.shape[0]
    n_parts, _, part = other.shape
    n_globs = len(globs) // 2

    @pl.when(pl.program_id(0) == 0)
    def _():
        row = where_ref[1] + lax.broadcasted_iota(jnp.int32, (size, gpos_ref.shape[1]), 0)
        hit = jnp.where(row == gpos_ref[...], 1.0, 0.0)
        is_glob = jnp.max(hit, axis=1, keepdims=True) > 0.0
        pick = hit.astype(BF16)

        def fixed(o_ref, parts, cols):
            rows = contract_last(pick, jnp.concatenate([g[0, cols, :] for g in parts], axis=1))
            return jnp.where(is_glob, rows, o_ref[:, cols].astype(F32)).astype(BF16)

        for i in range(n_parts):
            cols = slice(i * part, (i + 1) * part)
            mine[:, cols] = fixed(om_ref, globs[:n_globs], cols)
            other[i] = fixed(oo_ref, globs[n_globs:], cols)

    a_mine = jnp.dot(mine[...], wm_ref[...], preferred_element_type=F32)
    a_other = jnp.dot(other[where_ref[2]], w0_ref[...], preferred_element_type=F32)
    a_other = a_other + jnp.dot(other[where_ref[3]], w1_ref[...], preferred_element_type=F32)
    h_ref[...] = (x_ref[...].astype(F32) + (a_mine + a_other)).astype(BF16)


def hidden_block(where, gpos, o_mine, o_other, globs, x, wo_mine, wo_parts, local, size):
    heads, width = wo_mine.shape
    n_glob = gpos.shape[1]
    tile = 512
    n_parts = len(wo_parts)
    part = heads // n_parts
    return pl.pallas_call(
        hidden_kernel,
        out_shape=jax.ShapeDtypeStruct((size, width), BF16),
        grid_spec=pltpu.PrefetchScalarGridSpec(
            num_scalar_prefetch=1,
            grid=(width // tile,),
            in_specs=[
                pl.BlockSpec((1, n_glob), lambda j, r: (0, 0)),
                pl.BlockSpec((size, heads), lambda j, r: (local, 0)),
                pl.BlockSpec((size, heads), lambda j, r: (local, 0)),
                *[pl.BlockSpec((1, heads, n_glob // len(globs)), lambda j, r: (0, 0, 0))] * len(globs),
                *[pl.BlockSpec((1, heads, n_glob // len(globs)), lambda j, r: (1, 0, 0))] * len(globs),
                pl.BlockSpec((size, tile), lambda j, r: (r[0], j)),
                pl.BlockSpec((heads, tile), lambda j, r: (0, j)),
            ] + [pl.BlockSpec((part, tile), lambda j, r: (0, j))] * n_parts,
            out_specs=pl.BlockSpec((size, tile), lambda j, r: (0, j)),
            scratch_shapes=[pltpu.VMEM((size, heads), BF16), pltpu.VMEM((n_parts, size, part), BF16)],
        ),
        cost_estimate=pl.CostEstimate(flops=4 * size * heads * (width + n_glob), bytes_accessed=40 << 20, transcendentals=0),
        compiler_params=pltpu.CompilerParams(dimension_semantics=("arbitrary",), vmem_limit_bytes=62 << 20),
        name="hidden_rows",
    )(where, gpos, o_mine, o_other, *globs, *globs, x, wo_mine, *wo_parts)


def mlp_kernel(h_ref, up_ref, down_ref, o_ref):
    z = jnp.dot(h_ref[...], up_ref[...], preferred_element_type=F32)
    u = (0.5 * z * (1.0 + jnp.tanh(math.sqrt(2.0 / math.pi) * (z + 0.044715 * (z * z * z))))).astype(BF16)
    step = pl.program_id(0)

    @pl.when(step == 0)
    def _():
        o_ref[...] = jnp.dot(u, down_ref[...], preferred_element_type=F32)

    @pl.when(step > 0)
    def _():
        o_ref[...] += jnp.dot(u, down_ref[...], preferred_element_type=F32)


def mlp_block(h, w_up, w_down):
    size, width = h.shape
    inner = w_up.shape[1]
    tile = MLP_TILE
    return pl.pallas_call(
        mlp_kernel,
        out_shape=jax.ShapeDtypeStruct((size, width), F32),
        grid=(inner // tile,),
        in_specs=[
            pl.BlockSpec((size, width), lambda j: (0, 0)),
            pl.BlockSpec((width, tile), lambda j: (0, j)),
            pl.BlockSpec((tile, width), lambda j: (j, 0)),
        ],
        out_specs=pl.BlockSpec((size, width), lambda j: (0, 0)),
        cost_estimate=pl.CostEstimate(flops=4 * size * width * inner, bytes_accessed=4 * width * inner, transcendentals=size * inner),
        compiler_params=pltpu.CompilerParams(dimension_semantics=("arbitrary",), vmem_limit_bytes=62 << 20),
        name="mlp_rows",
    )(h, w_up, w_down)


def gate(value, *deps):
    return lax.optimization_barrier((value,) + deps)[0]


def solution(mesh):
    n_seq = mesh.shape['sp']
    to_right = [(i, i + 1) for i in range(n_seq - 1)]
    to_left = [(i + 1, i) for i in range(n_seq - 1)]
    swap = [(0, 1), (1, 0)]
    swap_core = [(i, i ^ 1) for i in range(n_seq)]
    swap_chip = [(i, i ^ 2) for i in range(n_seq)]

    def device_layer(tokens, glob_pos, w_query, w_key, w_value, w_out, w_up, w_down):
        n_rows, width = tokens.shape
        n_heads, dim = w_query.shape[1:]
        n_glob = glob_pos.shape[0]
        seq_len = n_rows * n_seq
        sp, tp = lax.axis_index('sp'), lax.axis_index('tp')
        first_row = sp * n_rows
        heads = n_heads * dim
        half = n_rows // 2
        away, home = (1 - tp) * half, tp * half
        quarters = [sp, sp ^ 2, sp ^ 1, sp ^ 3]

        share = n_glob // n_seq
        gpos = jnp.concatenate([lax.dynamic_slice_in_dim(glob_pos, q * share, share) for q in quarters])

        row_ids = first_row + jnp.arange(n_rows)
        pick = (gpos[:, None] == row_ids[None, :]).astype(BF16)
        picked = jnp.dot(pick, tokens, preferred_element_type=F32).astype(BF16)
        core = sp % 2
        chip_sum = picked[:2 * share] + lax.ppermute(picked[2 * share:], 'sp', swap_core)
        x_glob = chip_sum[:share] + lax.ppermute(chip_sum[share:], 'sp', swap_chip)

        wo_mine = w_out.reshape(heads, width)
        part = heads // 2
        wo_0 = lax.ppermute(lax.dynamic_slice_in_dim(wo_mine, core * part, part), 'tp', swap)
        wo_parts = (wo_0, lax.ppermute(wo_0, 'sp', swap_core))

        key_pos = first_row - WIN + jnp.arange(n_rows + 2 * WIN)
        key_glob = jnp.any(key_pos[:, None] == glob_pos[None, :], axis=1)
        key_ok = (key_pos >= 0) & (key_pos < seq_len) & jnp.logical_not(key_glob)
        bias = jnp.broadcast_to(jnp.where(key_ok, 0.0, -jnp.inf)[:, None], (n_rows + 2 * WIN, 128)).astype(F32)

        def project(rows, weight):
            return jnp.einsum('rd,dhe->hre', rows, weight, preferred_element_type=F32).astype(BF16)

        k_rows = project(gate(tokens, picked, bias), w_key)
        x_glob = gate(x_glob, k_rows)
        of_glob = jnp.stack([project(x_glob, w) for w in (w_key, w_value, w_query)])
        of_chip = lax.ppermute(of_glob, 'sp', swap_chip)
        of_core = lax.ppermute(of_glob, 'sp', swap_core)
        v_rows = project(gate(tokens, of_glob), w_value)
        left = lax.ppermute(jnp.stack([rows[:, n_rows - WIN:] for rows in (k_rows, v_rows)]), 'sp', to_right)
        right = lax.ppermute(jnp.stack([rows[:, :WIN] for rows in (k_rows, v_rows)]), 'sp', to_left)
        of_chip = gate(of_chip, v_rows)
        of_both = lax.ppermute(of_chip, 'sp', swap_core)
        of_globs = [of_glob, of_chip, of_core, of_both]

        def query_rows(start, *deps):
            return project(lax.dynamic_slice_in_dim(tokens, gate(start, *deps), half), w_query)

        q_home = query_rows(home, v_rows, of_chip)

        def window(start, q, block, *deps):
            row = gate((start + block * ROWS).reshape(1), *deps)
            return window_rows(row, q, block, k_rows, v_rows, left, right, of_globs, bias)

        att, att_other = {}, {}
        att['h0'] = window(home, q_home, 0)
        att_other['a0'] = lax.ppermute(att['h0'], 'tp', swap)

        mine = glob_part(of_globs[:1] + [gate(of_chip, att['h0'])] + of_globs[2:], k_rows, v_rows)
        parts = [mine[0]]
        for i in range(1, n_seq):
            flip = (0, 2, 1, 3)[i]
            parts.append(lax.ppermute(mine[i], 'sp', [(j, j ^ flip) for j in range(n_seq)]))
        att['h1'] = window(home, q_home, 1, mine[0])
        att_other['a1'] = lax.ppermute(att['h1'], 'tp', swap)
        q_away = query_rows(away, att['h1'])
        merged = merge_parts([gate(parts[0], q_away)] + parts[1:], dim).reshape(heads, share)
        merged_other = lax.ppermute(merged, 'tp', swap)
        att['a0'] = window(away, q_away, 0, merged)
        att_other['h0'] = lax.ppermute(att['a0'], 'tp', swap)
        glob = jnp.stack([merged, gate(merged_other, att['a0'])])
        glob_chip = lax.ppermute(glob, 'sp', swap_chip)
        glob_core = lax.ppermute(glob, 'sp', swap_core)
        att['a1'] = window(away, q_away, 1, att['a0'])
        att_other['h1'] = lax.ppermute(att['a1'], 'tp', swap)
        glob_chip = gate(glob_chip, att['a1'])
        globs = [glob, glob_chip, glob_core, lax.ppermute(glob_chip, 'sp', swap_core)]
        gpos = gpos.reshape(1, n_glob)

        def hidden_rows(key, start, offset, size, dep):
            row = start + offset
            where = jnp.stack([row // size, first_row + row, core, 1 - core]).astype(jnp.int32)
            return hidden_block(gate(where, dep), gpos, att[key], att_other[key], globs, tokens, wo_mine, wo_parts,
                                (offset % ROWS) // size, size)

        def mlp(h_blk):
            if h_blk.shape[0] < ROWS:
                return mlp_block(h_blk, w_up, w_down)
            u = jax.nn.gelu(jnp.dot(h_blk, w_up, preferred_element_type=F32), approximate=True).astype(BF16)
            return lax.optimization_barrier(jnp.dot(u, w_down, preferred_element_type=F32))

        sums, dep = [], att['a1']
        for key, offset, size in (('a0', 0, 256), ('a0', 256, 256), ('a1', 512, 512)):
            dep = partial = mlp(hidden_rows(key, away, offset, size, dep))
            sums.append(lax.ppermute(partial, 'tp', swap))

        def finish(h_blk, partial, total):
            return lax.optimization_barrier((h_blk.astype(F32) + (partial + total)).astype(BF16))

        pieces, y_other = [], []
        for c, arrived in ((0, sums[:2]), (1, [sums[2][:256], sums[2][256:]])):
            h_blk = hidden_rows('h%d' % c, home, c * ROWS, ROWS, dep)
            dep = partial = mlp(h_blk)
            size = ROWS // len(arrived)
            for i, total in enumerate(arrived):
                y = finish(h_blk[i * size:(i + 1) * size], partial[i * size:(i + 1) * size], gate(total, partial))
                y_other.append(lax.ppermute(y, 'tp', swap))
                pieces.append((y, c * ROWS + i * size))
        out = gate(jnp.zeros((n_rows, width), BF16), dep)
        for y, offset in pieces:
            out = lax.dynamic_update_slice_in_dim(out, y, home + offset, 0)
        for y, (_, offset) in zip(y_other, pieces):
            out = lax.dynamic_update_slice_in_dim(gate(out, pieces[-1][0]), y, away + offset, 0)
        return out

    row_spec = P(('dp', 'sp'), None)
    head_spec = P(None, 'tp', None)
    in_specs = (row_spec, P('dp'), head_spec, head_spec, head_spec, P('tp', None, None), P(None, 'tp'), P('tp', None))
    return jax.shard_map(device_layer, mesh=mesh, in_specs=in_specs, out_specs=row_spec, check_vma=False)
```

time: 1180 us -> 1060 us (0.90)
  matrix products: 524 us -> 413 us
  Pallas kernels: 267 us -> 345 us
  waiting for transfers between devices: 259 us -> 203 us
  other arithmetic: 43.1 us -> 26.6 us
    pallas_call x0 -> x2, Pallas kernels: none -> 91.4 us  [mlp_block(): pl.pallas_call(mlp_kernel, out_shape=jax.ShapeDtypeStruct((size, width),...]
    ppermute x1, waiting for transfers between devices: 58.2 us -> 0.01 us  [device_layer(): lax.ppermute(lax.dynamic_slice_in_dim(wo_mine, core * part, part), 'tp',...]
    dot_general x5 -> x3, matrix products: 173 us -> 120 us  [mlp(): jnp.dot(h_blk, w_up, preferred_element_type=F32)]
    dot_general x5 -> x3, matrix products: 165 us -> 116 us  [mlp(): jnp.dot(u, w_down, preferred_element_type=F32)]
    ppermute x3, waiting for transfers between devices: 0.01 us -> 21.3 us  [device_layer(): sums.append(lax.ppermute(partial, 'tp', swap))]
    ppermute x13 -> x14, waiting for transfers between devices: 39.3 us -> 23.9 us  [the longest x3 22.5 us: device_layer(): lax.ppermute(mine[i], 'sp', [(j, j ^ flip) for j in range(n_seq)])]
    pallas_call x4, Pallas kernels: 102 us -> 90.3 us  [window_rows(): pl.pallas_call(functools.partial(window_kernel, coef=LOG2E / math.sqrt(di...]
    dot_general x6 -> x7, matrix products: 170 us -> 165 us  [project(): jnp.einsum('rd,dhe->hre', rows, weight, preferred_element_type=F32)]
  transfers between devices with their start and end apart: 25 -> 27, of which waited for: 4 -> 8; matrix products, arithmetic and copies ran while one was open for 49% -> 43% of each run, Pallas kernels for 23% -> 33%
where the time goes in v2:
time: 1060 us; the launch traced here: 1050 us
  matrix products  413 us (39%)
  Pallas kernels  345 us (33%)
  waiting for transfers between devices  203 us (19%)
  local copies, waits for them, and re-layouts  36.6 us (3%)
  starting transfers between devices  27.2 us (3%)
  other arithmetic  26.6 us (3%)
    dot_general x7, matrix products, project(): jnp.einsum('rd,dhe->hre', rows, weight, preferred_element_type=F32)  165 us
    ppermute x4, waiting for transfers between devices, device_layer(): y_other.append(lax.ppermute(y, 'tp', swap))  158 us
    pallas_call x5, Pallas kernels, hidden_block(): pl.pallas_call(hidden_kernel, out_shape=jax.ShapeDtypeStruct((size, width...  129 us
    dot_general x3, matrix products, mlp(): jnp.dot(h_blk, w_up, preferred_element_type=F32)  120 us
    dot_general x3, matrix products, mlp(): jnp.dot(u, w_down, preferred_element_type=F32)  116 us
    pallas_call x2, Pallas kernels, mlp_block(): pl.pallas_call(mlp_kernel, out_shape=jax.ShapeDtypeStruct((size, width),...  91.4 us
    pallas_call x4, Pallas kernels, window_rows(): pl.pallas_call(functools.partial(window_kernel, coef=LOG2E / math.sqrt(di...  90.3 us
    pallas_call x1, Pallas kernels, glob_part(): pl.pallas_call(functools.partial(glob_kernel, coef=LOG2E / math.sqrt(dim)...  33.3 us
  transfers between devices with their start and end apart: 27, of which 8 were waited for; matrix products, arithmetic and copies ran while one was open for 43% of the time, Pallas kernels for 33%

profile of v2, /device:TPU:0, one launch (start us, length us, event | category | flops | bytes accessed | tf_op | source)
XLA Modules:
  0.0 1051.5 jit_solution(3674867115004433127)
XLA Ops:
  0.9 12.5 %convolution_convert_fusion = bf16[512,4096]{1,0:T(8,128)(2,1)S(1)} fusion(bf16[2048,4096]{1,0:T(8,128)(2,1)} %refs_8_.9, s32[2048]{0:T(1024)S(1)} %iota_add_fusion.1, s32[512]{0:T(512)S(1)} %pad_add_fusion), kind=kOutput, calls=%fused_computation.64 | convolution fusion | flops 8593080320 | bytes 20981760 | tf_op jit(solution)/shard_map/dot_general | solution.py:294
  13.4 2.0 copy-done.4
  16.4 7.8 constant_dynamic-slice_fusion
  24.2 2.5 collective-permute-start.15
  26.8 1.7 compare_reduce_fusion
  28.5 1.5 broadcast_in_dim.24.refs_8_
  30.1 2.4 slice_add_fusion.4
  33.6 1.5 collective-permute-start.1
  35.1 43.2 %convert_bitcast_fusion.1.k_ref.refs_4_ = bf16[16,2048,128]{2,1,0:T(8,128)(2,1)} fusion(bf16[4096,16,128]{2,1,0:T(8,128)(2,1)} %param.11, bf16[2048,4096]{1,0:T(8,128)(2,1)} %refs_8_.9), kind=kOutput, calls=%fused_computation.48 | convolution fusion | flops 34363932672 | bytes 41943040 | tf_op jit(solution)/shard_map/rd,dhe->hre/dot_general | solution.py:310
  78.5 8.9 fusion.101
  87.3 8.7 fusion.98
  96.1 10.5 %fusion.104 = bf16[1,16,128,128]{3,2,1,0:T(8,128)(2,1)S(1)} fusion(bf16[4096,16,128]{2,1,0:T(8,128)(2,1)S(1)} %bitcast.136, bf16[128,4096]{1,0:T(8,128)(2,1)S(1)} %slice_add_fusion.5), kind=kOutput, calls=%fused_computation.92 | convolution fusion | flops 2147745792 | bytes 18350080 | tf_op jit(solution)/shard_map/rd,dhe->hre/dot_general | solution.py:310
  107.4 42.8 %convert_bitcast_fusion.v_ref.refs_5_ = bf16[16,2048,128]{2,1,0:T(8,128)(2,1)} fusion(bf16[4096,16,128]{2,1,0:T(8,128)(2,1)} %param.12, bf16[2048,4096]{1,0:T(8,128)(2,1)} %refs_8_.9), kind=kOutput, calls=%fused_computation.47 | convolution fusion | flops 34363932672 | bytes 41943040 | tf_op jit(solution)/shard_map/rd,dhe->hre/dot_general | solution.py:310
  150.1 2.7 slice_bitcast_fusion
  152.8 1.5 pad_maximum_fusion
  154.3 3.5 collective-permute-start.3
  157.8 1.5 pad_maximum_fusion.1
  159.3 1.3 collective-permute-start.4
  160.6 1.1 collective-permute-start.6
  161.7 25.3 %convert_bitcast_fusion.3.q_ref = bf16[16,1024,128]{2,1,0:T(8,128)(2,1)} fusion(bf16[4096,16,128]{2,1,0:T(8,128)(2,1)} %param.10, bf16[2048,4096]{1,0:T(8,128)(2,1)} %refs_8_.9, s32[]{:T(128)S(6)} %select_n.87), kind=kOutput, calls=%fused_computation.79 | convolution fusion | flops 17181966336 | bytes 29360132 | tf_op jit(solution)/shard_map/rd,dhe->hre/dot_general | solution.py:310
  187.1 22.5 %window_attention.4.om_ref = bf16[512,2048]{1,0:T(8,128)(2,1)} custom-call(s32[1]{0:T(128)} %bitcast.25.r0_ref, bf16[16,1024,128]{2,1,0:T(8,128)(2,1)} %convert_bitcast_fusion.3.q_ref, bf16[16,2048,128]{2,1,0:T(8,128)(2,1)} %convert_bitcast_fusion.1.k_ref.refs_4_, bf16[16,2048,128]{2,1,0:T(8,128)(2,1)} %convert_bitcast_fusion.v_ref.refs_5_, ...), custom_call_target="tpu_custom_call" | custom-call | flops 10737418240 | bytes 29360128 | tf_op jit(solution)/shard_map/window_attention/pallas_call | solution.py:91
  209.8 33.3 %global_queries.1 = (f32[16,136,128]{2,1,0:T(8,128)}, f32[16,136,128]{2,1,0:T(8,128)}, f32[16,136,128]{2,1,0:T(8,128)}, f32[16,136,128]{2,1,0:T(8,128)}) custom-call(bf16[3,16,128,128]{3,2,1,0:T(8,128)(2,1)} %copy-done, bf16[3,16,128,128]{3,2,1,0:T(8,128)(2,1)} %collective-permute-done.2.refs_1_.refs_5_, ...), custom_call_target="tpu_custom_call" | custom-call | flops 17179869184 | bytes 25165824 | tf_op jit(solution)/shard_map/global_queries/pallas_call | solution.py:153
  243.1 22.4 %window_attention.5.om_ref = bf16[512,2048]{1,0:T(8,128)(2,1)} custom-call(s32[1]{0:T(128)} %bitcast.32.r0_ref, bf16[16,1024,128]{2,1,0:T(8,128)(2,1)} %convert_bitcast_fusion.3.q_ref, bf16[16,2048,128]{2,1,0:T(8,128)(2,1)} %convert_bitcast_fusion.1.k_ref.refs_4_, bf16[16,2048,128]{2,1,0:T(8,128)(2,1)} %convert_bitcast_fusion.v_ref.refs_5_, ...), custom_call_target="tpu_custom_call" | custom-call | flops 10737418240 | bytes 29360128 | tf_op jit(solution)/shard_map/window_attention/pallas_call | solution.py:91
  265.6 1.7 collective-permute-start.7
  267.8 25.2 %convert_bitcast_fusion.2.q_ref = bf16[16,1024,128]{2,1,0:T(8,128)(2,1)} fusion(bf16[4096,16,128]{2,1,0:T(8,128)(2,1)} %param.10, bf16[2048,4096]{1,0:T(8,128)(2,1)} %refs_8_.9, s32[]{:T(128)S(6)} %select_n.88), kind=kOutput, calls=%fused_computation.78 | convolution fusion | flops 17181966336 | bytes 29360132 | tf_op jit(solution)/shard_map/rd,dhe->hre/dot_general | solution.py:310
  293.3 22.2 %collective-permute-done.9 = f32[16,136,128]{2,1,0:T(8,128)S(1)} collective-permute-done((f32[16,136,128]{2,1,0:T(8,128)}, f32[16,136,128]{2,1,0:T(8,128)S(1)}, u32[]{:S(2)}, u32[]{:S(2)}) %collective-permute-start.9) | collective-permute-done | bytes 1114144 | tf_op jit(solution)/shard_map/ppermute | solution.py:341
  316.5 1.6 fusion.108
  318.2 1.5 collective-permute-start.11
  319.7 22.9 %window_attention.6.om_ref = bf16[512,2048]{1,0:T(8,128)(2,1)} custom-call(s32[1]{0:T(128)} %bitcast.13.r0_ref, bf16[16,1024,128]{2,1,0:T(8,128)(2,1)} %convert_bitcast_fusion.2.q_ref, bf16[16,2048,128]{2,1,0:T(8,128)(2,1)} %convert_bitcast_fusion.1.k_ref.refs_4_, bf16[16,2048,128]{2,1,0:T(8,128)(2,1)} %convert_bitcast_fusion.v_ref.refs_5_, ...), custom_call_target="tpu_custom_call" | custom-call | flops 10737418240 | bytes 29360128 | tf_op jit(solution)/shard_map/window_attention/pallas_call | solution.py:91
  344.6 1.4 collective-permute-start.12
  346.0 22.5 %window_attention.7.om_ref = bf16[512,2048]{1,0:T(8,128)(2,1)} custom-call(s32[1]{0:T(128)} %bitcast.12.r0_ref, bf16[16,1024,128]{2,1,0:T(8,128)(2,1)} %convert_bitcast_fusion.2.q_ref, bf16[16,2048,128]{2,1,0:T(8,128)(2,1)} %convert_bitcast_fusion.1.k_ref.refs_4_, bf16[16,2048,128]{2,1,0:T(8,128)(2,1)} %convert_bitcast_fusion.v_ref.refs_5_, ...), custom_call_target="tpu_custom_call" | custom-call | flops 10737418240 | bytes 29360128 | tf_op jit(solution)/shard_map/window_attention/pallas_call | solution.py:91
  368.8 1.4 collective-permute-done.12.refs_1_.refs_5_
  372.6 1.5 collective-permute-start.19
  375.6 21.5 %hidden_rows.5.h_ref = bf16[256,4096]{1,0:T(8,128)(2,1)} custom-call(s32[4]{0:T(128)} %add_add_fusion.4.where_ref, s32[1,512]{1,0:T(1,128)} %bitcast.130, bf16[512,2048]{1,0:T(8,128)(2,1)} %window_attention.6.om_ref, bf16[512,2048]{1,0:T(8,128)(2,1)} %collective-permute-done.10.oo_ref, bf16[2,2048,128]{2,1,0:T(8,128)(2,1)} %copy-done.1, ...), custom_call_target="tpu_custom_call" | custom-call | flops 9663676416 | bytes 41943040 | tf_op jit(solution)/shard_map/hidden_rows/pallas_call | solution.py:207
  397.1 45.7 %mlp_rows.2 = f32[256,4096]{1,0:T(8,128)} custom-call(bf16[256,4096]{1,0:T(8,128)(2,1)} %hidden_rows.5.h_ref, bf16[4096,7168]{1,0:T(8,128)(2,1)} %up_ref.3, bf16[7168,4096]{1,0:T(8,128)(2,1)} %down_ref.3), custom_call_target="tpu_custom_call" | custom-call | flops 30064771072 | bytes 117440512 | tf_op jit(solution)/shard_map/mlp_rows/pallas_call | solution.py:249
  442.8 1.5 collective-permute-start.20
  444.4 21.5 %hidden_rows.6.h_ref = bf16[256,4096]{1,0:T(8,128)(2,1)} custom-call(s32[4]{0:T(128)} %get-tuple-element.54.where_ref, s32[1,512]{1,0:T(1,128)} %bitcast.131, bf16[512,2048]{1,0:T(8,128)(2,1)} %window_attention.6.om_ref, bf16[512,2048]{1,0:T(8,128)(2,1)} %collective-permute-done.10.oo_ref, bf16[2,2048,128]{2,1,0:T(8,128)(2,1)} %copy-done.1, ...), custom_call_target="tpu_custom_call" | custom-call | flops 9663676416 | bytes 41943040 | tf_op jit(solution)/shard_map/hidden_rows/pallas_call | solution.py:207
  465.9 45.7 %mlp_rows.3 = f32[256,4096]{1,0:T(8,128)} custom-call(bf16[256,4096]{1,0:T(8,128)(2,1)} %hidden_rows.6.h_ref, bf16[4096,7168]{1,0:T(8,128)(2,1)} %up_ref.3, bf16[7168,4096]{1,0:T(8,128)(2,1)} %down_ref.3), custom_call_target="tpu_custom_call" | custom-call | flops 30064771072 | bytes 117440512 | tf_op jit(solution)/shard_map/mlp_rows/pallas_call | solution.py:249
  512.1 28.7 %hidden_rows.7 = bf16[512,4096]{1,0:T(8,128)(2,1)} custom-call(s32[4]{0:T(128)} %get-tuple-element.55.where_ref, s32[1,512]{1,0:T(1,128)} %bitcast.132, bf16[512,2048]{1,0:T(8,128)(2,1)} %window_attention.7.om_ref, bf16[512,2048]{1,0:T(8,128)(2,1)} %collective-permute-done.17.oo_ref, bf16[2,2048,128]{2,1,0:T(8,128)(2,1)} %copy-done.1, ...), custom_call_target="tpu_custom_call" | custom-call | flops 19327352832 | bytes 41943040 | tf_op jit(solution)/shard_map/hidden_rows/pallas_call | solution.py:207
  540.8 39.7 %fusion.165 = bf16[512,7168]{1,0:T(8,128)(2,1)S(1)} fusion(bf16[512,4096]{1,0:T(8,128)(2,1)} %hidden_rows.7, bf16[4096,7168]{1,0:T(8,128)(2,1)} %up_ref.3), kind=kOutput, calls=%fused_computation.20.clone.clone | convolution fusion | flops 30097801216 | bytes 70254592 | tf_op jit(solution)/shard_map/dot_general | solution.py:367
  580.4 38.0 %fusion.48 = f32[512,4096]{1,0:T(8,128)} fusion(bf16[7168,4096]{1,0:T(8,128)(2,1)} %down_ref.3, bf16[512,7168]{1,0:T(8,128)(2,1)S(1)} %fusion.165), kind=kOutput, calls=%fused_computation.51 | convolution fusion | flops 30064771072 | bytes 74448896 | tf_op jit(solution)/shard_map/dot_general | solution.py:368
  618.4 1.6 collective-permute-start.22
  619.9 29.0 %hidden_rows.8 = bf16[512,4096]{1,0:T(8,128)(2,1)} custom-call(s32[4]{0:T(128)} %get-tuple-element.56.where_ref, s32[1,512]{1,0:T(1,128)} %bitcast.133, bf16[512,2048]{1,0:T(8,128)(2,1)} %window_attention.4.om_ref, bf16[512,2048]{1,0:T(8,128)(2,1)} %collective-permute-done.18.oo_ref, bf16[2,2048,128]{2,1,0:T(8,128)(2,1)} %copy-done.1, ...), custom_call_target="tpu_custom_call" | custom-call | flops 19327352832 | bytes 41943040 | tf_op jit(solution)/shard_map/hidden_rows/pallas_call | solution.py:207
  648.9 39.3 %fusion.161 = bf16[512,7168]{1,0:T(8,128)(2,1)S(1)} fusion(bf16[512,4096]{1,0:T(8,128)(2,1)} %hidden_rows.8, bf16[4096,7168]{1,0:T(8,128)(2,1)} %up_ref.3), kind=kOutput, calls=%fused_computation.28.clone.clone | convolution fusion | flops 30097801216 | bytes 70254592 | tf_op jit(solution)/shard_map/dot_general | solution.py:367
  688.2 38.2 %fusion.46 = f32[512,4096]{1,0:T(8,128)} fusion(bf16[7168,4096]{1,0:T(8,128)(2,1)} %down_ref.3, bf16[512,7168]{1,0:T(8,128)(2,1)S(1)} %fusion.161), kind=kOutput, calls=%fused_computation.50 | convolution fusion | flops 30064771072 | bytes 74448896 | tf_op jit(solution)/shard_map/dot_general | solution.py:368
  726.4 28.8 %hidden_rows.9 = bf16[512,4096]{1,0:T(8,128)(2,1)} custom-call(s32[4]{0:T(128)} %get-tuple-element.57.where_ref, s32[1,512]{1,0:T(1,128)} %bitcast.134, bf16[512,2048]{1,0:T(8,128)(2,1)} %window_attention.5.om_ref, bf16[512,2048]{1,0:T(8,128)(2,1)} %collective-permute-done.19.oo_ref, bf16[2,2048,128]{2,1,0:T(8,128)(2,1)} %copy-done.1, ...), custom_call_target="tpu_custom_call" | custom-call | flops 19327352832 | bytes 41943040 | tf_op jit(solution)/shard_map/hidden_rows/pallas_call | solution.py:207
  755.1 40.9 %fusion.157 = bf16[512,7168]{1,0:T(8,128)(2,1)} fusion(bf16[512,4096]{1,0:T(8,128)(2,1)} %hidden_rows.9, bf16[4096,7168]{1,0:T(8,128)(2,1)} %up_ref.3), kind=kOutput, calls=%fused_computation.36.clone.clone.1 | convolution fusion | flops 30097801216 | bytes 70254592 | tf_op jit(solution)/shard_map/dot_general | solution.py:367
  796.1 39.7 %fusion.44 = f32[512,4096]{1,0:T(8,128)} fusion(bf16[7168,4096]{1,0:T(8,128)(2,1)} %down_ref.3, bf16[512,7168]{1,0:T(8,128)(2,1)} %fusion.157), kind=kOutput, calls=%fused_computation.49 | convolution fusion | flops 30064771072 | bytes 74448896 | tf_op jit(solution)/shard_map/dot_general | solution.py:368
  835.8 7.4 fusion.75
  843.7 1.5 collective-permute-start.24
  845.2 1.9 broadcast_in_dim.12
  847.1 1.9 constant_dynamic-update-slice_fusion.7
  849.0 21.3 %collective-permute-done.22 = f32[512,4096]{1,0:T(8,128)} collective-permute-done((f32[512,4096]{1,0:T(8,128)}, f32[512,4096]{1,0:T(8,128)}, u32[]{:S(2)}, u32[]{:S(2)}) %collective-permute-start.22) | collective-permute-done | bytes 8388640 | tf_op jit(solution)/shard_map/ppermute | solution.py:373
  870.3 6.2 fusion.129
  876.6 6.9 fusion.71
  884.0 1.8 constant_dynamic-update-slice_fusion.6
  885.8 1.6 collective-permute-start.26
  887.9 27.3 %collective-permute-done.23 = bf16[256,4096]{1,0:T(8,128)(2,1)} collective-permute-done((bf16[256,4096]{1,0:T(8,128)(2,1)}, bf16[256,4096]{1,0:T(8,128)(2,1)}, u32[]{:S(2)}, u32[]{:S(2)}) %collective-permute-start.23) | collective-permute-done | bytes 2097184 | tf_op jit(solution)/shard_map/ppermute | solution.py:385
  915.3 1.8 constant_dynamic-update-slice_fusion.3
  917.1 43.1 %collective-permute-done.24 = bf16[256,4096]{1,0:T(8,128)(2,1)} collective-permute-done((bf16[256,4096]{1,0:T(8,128)(2,1)}, bf16[256,4096]{1,0:T(8,128)(2,1)}, u32[]{:S(2)}, u32[]{:S(2)}) %collective-permute-start.24) | collective-permute-done | bytes 2097184 | tf_op jit(solution)/shard_map/ppermute | solution.py:385
  960.2 1.8 constant_dynamic-update-slice_fusion.2
  962.1 43.0 %collective-permute-done.25 = bf16[256,4096]{1,0:T(8,128)(2,1)S(1)} collective-permute-done((bf16[256,4096]{1,0:T(8,128)(2,1)S(1)}, bf16[256,4096]{1,0:T(8,128)(2,1)S(1)}, u32[]{:S(2)}, u32[]{:S(2)}) %collective-permute-start.25) | collective-permute-done | bytes 2097184 | tf_op jit(solution)/shard_map/ppermute | solution.py:385
  1005.3 44.2 %collective-permute-done.26 = bf16[256,4096]{1,0:T(8,128)(2,1)S(1)} collective-permute-done((bf16[256,4096]{1,0:T(8,128)(2,1)S(1)}, bf16[256,4096]{1,0:T(8,128)(2,1)S(1)}, u32[]{:S(2)}, u32[]{:S(2)}) %collective-permute-start.26) | collective-permute-done | bytes 2097184 | tf_op jit(solution)/shard_map/ppermute | solution.py:385
  1049.5 1.5 constant_dynamic-update-slice_fusion
  (86 shorter events, 14.4 us)
Async XLA Ops:
  0.9 12.5 %copy-start.8 = (s32[512]{0:T(512)}, s32[512]{0:T(512)S(1)}, u32[]{:S(2)}) copy-start(s32[512]{0:T(512)S(1)} %pad_add_fusion) | copy-start | bytes 6148
  13.4 2.0 copy-start.4
  15.6 14.5 %collective-permute-start = (bf16[256,4096]{1,0:T(8,128)(2,1)S(1)}, bf16[256,4096]{1,0:T(8,128)(2,1)}, u32[]{:S(2)}, u32[]{:S(2)}) collective-permute-start(bf16[256,4096]{1,0:T(8,128)(2,1)S(1)} %slice.121), channel_id=1, source_target_pairs={{0,1},{1,0},{2,3},{3,2},{4,5},{5,4},{6,7},{7,6}} | collective-permute-start | bytes 6291464 | tf_op jit(solution)/shard_map/ppermute | solution.py:296
  16.4 10.3 copy-start.9
  24.2 243.5 %collective-permute-start.15 = (bf16[1024,4096]{1,0:T(8,128)(2,1)}, bf16[1024,4096]{1,0:T(8,128)(2,1)}, u32[]{:S(2)}, u32[]{:S(2)}) collective-permute-start(bf16[1024,4096]{1,0:T(8,128)(2,1)} %constant_dynamic-slice_fusion), channel_id=1, source_target_pairs={{0,4},{4,0},{1,5},{5,1},{2,6},{6,2},{3,7},{7,3}} | collective-permute-start | bytes 25165832 | tf_op jit(solution)/shard_map/ppermute | solution.py:301
  33.6 44.7 %collective-permute-start.1 = (bf16[128,4096]{1,0:T(8,128)(2,1)}, bf16[128,4096]{1,0:T(8,128)(2,1)S(1)}, u32[]{:S(2)}, u32[]{:S(2)}) collective-permute-start(bf16[128,4096]{1,0:T(8,128)(2,1)} %slice.123), channel_id=1, source_target_pairs={{0,2},{1,3},{2,0},{3,1},{4,6},{5,7},{6,4},{7,5}} | collective-permute-start | bytes 3145736 | tf_op jit(solution)/shard_map/ppermute | solution.py:297
  78.4 17.6 %slice-start.2 = ((s8[16777216]{0:T(1024)(128)(4,1)}), s8[4194304]{0:T(1024)(128)(4,1)S(1)}, s32[]{:S(2)}) async-start(s8[16777216]{0:T(1024)(128)(4,1)} %bitcast.135), calls=%async_computation.2 | async-start | bytes 8388608
  78.4 17.6 %slice-start.3 = ((s8[16777216]{0:T(1024)(128)(4,1)}), s8[4194304]{0:T(1024)(128)(4,1)S(1)}, s32[]{:S(2)}) async-start(s8[16777216]{0:T(1024)(128)(4,1)} %bitcast.135), calls=%async_computation.3 | async-start | bytes 8388608
  78.4 17.6 %slice-start.4 = ((s8[16777216]{0:T(1024)(128)(4,1)}), s8[4194304]{0:T(1024)(128)(4,1)S(1)}, s32[]{:S(2)}) async-start(s8[16777216]{0:T(1024)(128)(4,1)} %bitcast.135), calls=%async_computation.4 | async-start | bytes 8388608
  87.3 8.7 slice-start.5
  106.8 43.3 %copy-start = (bf16[3,16,128,128]{3,2,1,0:T(8,128)(2,1)}, bf16[3,16,128,128]{3,2,1,0:T(8,128)(2,1)S(1)}, u32[]{:S(2)}) copy-start(bf16[3,16,128,128]{3,2,1,0:T(8,128)(2,1)S(1)} %pad_maximum_fusion.2.refs_0_.refs_4_) | copy-start | bytes 4718596
  106.8 80.3 %collective-permute-start.5 = (bf16[3,16,128,128]{3,2,1,0:T(8,128)(2,1)S(1)}, bf16[3,16,128,128]{3,2,1,0:T(8,128)(2,1)}, u32[]{:S(2)}, u32[]{:S(2)}) collective-permute-start(bf16[3,16,128,128]{3,2,1,0:T(8,128)(2,1)S(1)} %pad_maximum_fusion.2.refs_0_.refs_4_), channel_id=1, source_target_pairs={{0,1},{1,0},{2,3},{3,2},{4,5},{5,4},{6,7},{7,6}} | collective-permute-start | bytes 4718600 | tf_op jit(solution)/shard_map/ppermute | solution.py:316
  106.8 53.7 %collective-permute-start.2 = (bf16[3,16,128,128]{3,2,1,0:T(8,128)(2,1)S(1)}, bf16[3,16,128,128]{3,2,1,0:T(8,128)(2,1)}, u32[]{:S(2)}, u32[]{:S(2)}) collective-permute-start(bf16[3,16,128,128]{3,2,1,0:T(8,128)(2,1)S(1)} %pad_maximum_fusion.2.refs_0_.refs_4_), channel_id=1, source_target_pairs={{0,2},{1,3},{2,0},{3,1},{4,6},{5,7},{6,4},{7,5}} | collective-permute-start | bytes 4718600 | tf_op jit(solution)/shard_map/ppermute | solution.py:315
  154.3 32.8 %collective-permute-start.3 = (bf16[2,16,256,128]{3,2,1,0:T(8,128)(2,1)}, bf16[2,16,256,128]{3,2,1,0:T(8,128)(2,1)}, u32[]{:S(2)}, u32[]{:S(2)}) collective-permute-start(bf16[2,16,256,128]{3,2,1,0:T(8,128)(2,1)} %pad_maximum_fusion), channel_id=1, source_target_pairs={{0,1},{1,2},{2,3},{4,5},{5,6},{6,7}} | collective-permute-start | bytes 6291464 | tf_op jit(solution)/shard_map/ppermute | solution.py:318
  159.3 27.8 %collective-permute-start.4 = (bf16[2,16,256,128]{3,2,1,0:T(8,128)(2,1)}, bf16[2,16,256,128]{3,2,1,0:T(8,128)(2,1)}, u32[]{:S(2)}, u32[]{:S(2)}) collective-permute-start(bf16[2,16,256,128]{3,2,1,0:T(8,128)(2,1)} %pad_maximum_fusion.1), channel_id=1, source_target_pairs={{1,0},{2,1},{3,2},{5,4},{6,5},{7,6}} | collective-permute-start | bytes 6291464 | tf_op jit(solution)/shard_map/ppermute | solution.py:319
  160.6 26.5 %collective-permute-start.6 = (bf16[3,16,128,128]{3,2,1,0:T(8,128)(2,1)}, bf16[3,16,128,128]{3,2,1,0:T(8,128)(2,1)}, u32[]{:S(2)}, u32[]{:S(2)}) collective-permute-start(bf16[3,16,128,128]{3,2,1,0:T(8,128)(2,1)} %collective-permute-done.2.refs_1_.refs_5_), channel_id=1, source_target_pairs={{0,1},{1,0},{2,3},{3,2},{4,5},{5,4},{6,7},{7,6}} | collective-permute-start | bytes 4718600 | tf_op jit(solution)/shard_map/ppermute | solution.py:321
  209.6 163.0 %collective-permute-start.10 = (bf16[512,2048]{1,0:T(8,128)(2,1)}, bf16[512,2048]{1,0:T(8,128)(2,1)}, u32[]{:S(2)}, u32[]{:S(2)}) collective-permute-start(bf16[512,2048]{1,0:T(8,128)(2,1)} %window_attention.4.om_ref), channel_id=1, source_target_pairs={{0,4},{4,0},{1,5},{5,1},{2,6},{6,2},{3,7},{7,3}} | collective-permute-start | bytes 6291464 | tf_op jit(solution)/shard_map/ppermute | solution.py:335
  265.6 27.7 %collective-permute-start.7 = (f32[16,136,128]{2,1,0:T(8,128)}, f32[16,136,128]{2,1,0:T(8,128)S(1)}, u32[]{:S(2)}, u32[]{:S(2)}) collective-permute-start(f32[16,136,128]{2,1,0:T(8,128)} %get-tuple-element.46), channel_id=1, source_target_pairs={{0,2},{1,3},{2,0},{3,1},{4,6},{5,7},{6,4},{7,5}} | collective-permute-start | bytes 3342344 | tf_op jit(solution)/shard_map/ppermute | solution.py:341
  267.3 26.0 %collective-permute-start.8 = (f32[16,136,128]{2,1,0:T(8,128)}, f32[16,136,128]{2,1,0:T(8,128)S(1)}, u32[]{:S(2)}, u32[]{:S(2)}) collective-permute-start(f32[16,136,128]{2,1,0:T(8,128)} %get-tuple-element.47), channel_id=1, source_target_pairs={{0,1},{1,0},{2,3},{3,2},{4,5},{5,4},{6,7},{7,6}} | collective-permute-start | bytes 3342344 | tf_op jit(solution)/shard_map/ppermute | solution.py:341
  267.3 48.2 %collective-permute-start.9 = (f32[16,136,128]{2,1,0:T(8,128)}, f32[16,136,128]{2,1,0:T(8,128)S(1)}, u32[]{:S(2)}, u32[]{:S(2)}) collective-permute-start(f32[16,136,128]{2,1,0:T(8,128)} %get-tuple-element.48), channel_id=1, source_target_pairs={{0,3},{1,2},{2,1},{3,0},{4,7},{5,6},{6,5},{7,4}} | collective-permute-start | bytes 3342344 | tf_op jit(solution)/shard_map/ppermute | solution.py:341
  267.8 47.8 %copy-start.6 = (f32[16,136,128]{2,1,0:T(8,128)S(1)}, f32[16,136,128]{2,1,0:T(8,128)}, u32[]{:S(2)}) copy-start(f32[16,136,128]{2,1,0:T(8,128)} %get-tuple-element.45) | copy-start | bytes 3342340
  267.8 107.8 %collective-permute-start.16 = (bf16[1024,4096]{1,0:T(8,128)(2,1)}, bf16[1024,4096]{1,0:T(8,128)(2,1)}, u32[]{:S(2)}, u32[]{:S(2)}) collective-permute-start(bf16[1024,4096]{1,0:T(8,128)(2,1)} %collective-permute-done.15.refs_10_), channel_id=1, source_target_pairs={{0,1},{1,0},{2,3},{3,2},{4,5},{5,4},{6,7},{7,6}} | collective-permute-start | bytes 25165832 | tf_op jit(solution)/shard_map/ppermute | solution.py:302
  315.5 1.0 copy-start.5
  318.2 24.4 %collective-permute-start.11 = (bf16[2048,128]{1,0:T(8,128)(2,1)S(1)}, bf16[2048,128]{1,0:T(8,128)(2,1)S(1)}, u32[]{:S(2)}, u32[]{:S(2)}) collective-permute-start(bf16[2048,128]{1,0:T(8,128)(2,1)S(1)} %bitcast.119), channel_id=1, source_target_pairs={{0,4},{4,0},{1,5},{5,1},{2,6},{6,2},{3,7},{7,3}} | collective-permute-start | bytes 1572872 | tf_op jit(solution)/shard_map/ppermute | solution.py:346
  342.6 0.8 copy-start.7
  344.6 23.9 %copy-start.1 = (bf16[2,2048,128]{2,1,0:T(8,128)(2,1)}, bf16[2,2048,128]{2,1,0:T(8,128)(2,1)S(1)}, u32[]{:S(2)}) copy-start(bf16[2,2048,128]{2,1,0:T(8,128)(2,1)S(1)} %pad_maximum_fusion.3.refs_0_.refs_4_) | copy-start | bytes 3145732
  344.6 25.6 %collective-permute-start.12 = (bf16[2,2048,128]{2,1,0:T(8,128)(2,1)S(1)}, bf16[2,2048,128]{2,1,0:T(8,128)(2,1)}, u32[]{:S(2)}, u32[]{:S(2)}) collective-permute-start(bf16[2,2048,128]{2,1,0:T(8,128)(2,1)S(1)} %pad_maximum_fusion.3.refs_0_.refs_4_), channel_id=1, source_target_pairs={{0,2},{1,3},{2,0},{3,1},{4,6},{5,7},{6,4},{7,5}} | collective-permute-start | bytes 3145736 | tf_op jit(solution)/shard_map/ppermute | solution.py:350
  368.5 5.7 collective-permute-start.13
  370.2 5.4 collective-permute-start.14
  372.1 140.0 %collective-permute-start.17 = (bf16[512,2048]{1,0:T(8,128)(2,1)}, bf16[512,2048]{1,0:T(8,128)(2,1)}, u32[]{:S(2)}, u32[]{:S(2)}) collective-permute-start(bf16[512,2048]{1,0:T(8,128)(2,1)} %window_attention.5.om_ref), channel_id=1, source_target_pairs={{0,4},{4,0},{1,5},{5,1},{2,6},{6,2},{3,7},{7,3}} | collective-permute-start | bytes 6291464 | tf_op jit(solution)/shard_map/ppermute | solution.py:343
  372.6 353.8 %collective-permute-start.19 = (bf16[512,2048]{1,0:T(8,128)(2,1)}, bf16[512,2048]{1,0:T(8,128)(2,1)}, u32[]{:S(2)}, u32[]{:S(2)}) collective-permute-start(bf16[512,2048]{1,0:T(8,128)(2,1)} %window_attention.7.om_ref), channel_id=1, source_target_pairs={{0,4},{4,0},{1,5},{5,1},{2,6},{6,2},{3,7},{7,3}} | collective-permute-start | bytes 6291464 | tf_op jit(solution)/shard_map/ppermute | solution.py:353
  374.1 1.0 copy-start.2
  375.1 244.8 %collective-permute-start.18 = (bf16[512,2048]{1,0:T(8,128)(2,1)}, bf16[512,2048]{1,0:T(8,128)(2,1)}, u32[]{:S(2)}, u32[]{:S(2)}) collective-permute-start(bf16[512,2048]{1,0:T(8,128)(2,1)} %window_attention.6.om_ref), channel_id=1, source_target_pairs={{0,4},{4,0},{1,5},{5,1},{2,6},{6,2},{3,7},{7,3}} | collective-permute-start | bytes 6291464 | tf_op jit(solution)/shard_map/ppermute | solution.py:348
  442.8 392.9 %collective-permute-start.20 = (f32[256,4096]{1,0:T(8,128)}, f32[256,4096]{1,0:T(8,128)}, u32[]{:S(2)}, u32[]{:S(2)}) collective-permute-start(f32[256,4096]{1,0:T(8,128)} %mlp_rows.2), channel_id=1, source_target_pairs={{0,4},{4,0},{1,5},{5,1},{2,6},{6,2},{3,7},{7,3}} | collective-permute-start | bytes 12582920 | tf_op jit(solution)/shard_map/ppermute | solution.py:373
  511.6 324.2 %collective-permute-start.21 = (f32[256,4096]{1,0:T(8,128)}, f32[256,4096]{1,0:T(8,128)}, u32[]{:S(2)}, u32[]{:S(2)}) collective-permute-start(f32[256,4096]{1,0:T(8,128)} %mlp_rows.3), channel_id=1, source_target_pairs={{0,4},{4,0},{1,5},{5,1},{2,6},{6,2},{3,7},{7,3}} | collective-permute-start | bytes 12582920 | tf_op jit(solution)/shard_map/ppermute | solution.py:373
  618.4 251.9 %collective-permute-start.22 = (f32[512,4096]{1,0:T(8,128)}, f32[512,4096]{1,0:T(8,128)}, u32[]{:S(2)}, u32[]{:S(2)}) collective-permute-start(f32[512,4096]{1,0:T(8,128)} %fusion.48), channel_id=1, source_target_pairs={{0,4},{4,0},{1,5},{5,1},{2,6},{6,2},{3,7},{7,3}} | collective-permute-start | bytes 25165832 | tf_op jit(solution)/shard_map/ppermute | solution.py:373
  755.1 80.6 %slice-start = ((s8[8388608]{0:T(1024)(128)(4,1)}), s8[4194304]{0:T(1024)(128)(4,1)S(1)}, s32[]{:S(2)}) async-start(s8[8388608]{0:T(1024)(128)(4,1)} %bitcast.117), calls=%async_computation | async-start | bytes 8388608
  796.1 39.7 %slice-start.1 = ((s8[8388608]{0:T(1024)(128)(4,1)}), s8[4194304]{0:T(1024)(128)(4,1)S(1)}, s32[]{:S(2)}) async-start(s8[8388608]{0:T(1024)(128)(4,1)} %bitcast.117), calls=%async_computation.1 | async-start | bytes 8388608
  843.2 72.1 %collective-permute-start.23 = (bf16[256,4096]{1,0:T(8,128)(2,1)}, bf16[256,4096]{1,0:T(8,128)(2,1)}, u32[]{:S(2)}, u32[]{:S(2)}) collective-permute-start(bf16[256,4096]{1,0:T(8,128)(2,1)} %get-tuple-element.77), channel_id=1, source_target_pairs={{0,4},{4,0},{1,5},{5,1},{2,6},{6,2},{3,7},{7,3}} | collective-permute-start | bytes 6291464 | tf_op jit(solution)/shard_map/ppermute | solution.py:385
  843.7 116.5 %collective-permute-start.24 = (bf16[256,4096]{1,0:T(8,128)(2,1)}, bf16[256,4096]{1,0:T(8,128)(2,1)}, u32[]{:S(2)}, u32[]{:S(2)}) collective-permute-start(bf16[256,4096]{1,0:T(8,128)(2,1)} %get-tuple-element.76), channel_id=1, source_target_pairs={{0,4},{4,0},{1,5},{5,1},{2,6},{6,2},{3,7},{7,3}} | collective-permute-start | bytes 6291464 | tf_op jit(solution)/shard_map/ppermute | solution.py:385
  883.5 121.6 %collective-permute-start.25 = (bf16[256,4096]{1,0:T(8,128)(2,1)S(1)}, bf16[256,4096]{1,0:T(8,128)(2,1)S(1)}, u32[]{:S(2)}, u32[]{:S(2)}) collective-permute-start(bf16[256,4096]{1,0:T(8,128)(2,1)S(1)} %get-tuple-element.75), channel_id=1, source_target_pairs={{0,4},{4,0},{1,5},{5,1},{2,6},{6,2},{3,7},{7,3}} | collective-permute-start | bytes 6291464 | tf_op jit(solution)/shard_map/ppermute | solution.py:385
  885.8 163.7 %collective-permute-start.26 = (bf16[256,4096]{1,0:T(8,128)(2,1)S(1)}, bf16[256,4096]{1,0:T(8,128)(2,1)S(1)}, u32[]{:S(2)}, u32[]{:S(2)}) collective-permute-start(bf16[256,4096]{1,0:T(8,128)(2,1)S(1)} %get-tuple-element.74), channel_id=1, source_target_pairs={{0,4},{4,0},{1,5},{5,1},{2,6},{6,2},{3,7},{7,3}} | collective-permute-start | bytes 6291464 | tf_op jit(solution)/shard_map/ppermute | solution.py:385
  1005.3 44.2 %copy-start.3 = (bf16[2048,4096]{1,0:T(8,128)(2,1)}, bf16[2048,4096]{1,0:T(8,128)(2,1)S(1)}, u32[]{:S(2)}) copy-start(bf16[2048,4096]{1,0:T(8,128)(2,1)S(1)} %constant_dynamic-update-slice_fusion.1) | copy-start | bytes 50331652

commit v3 on v2

--- a/solution.py
+++ b/solution.py
@@ -111,8 +111,8 @@
             ],
         ),
         cost_estimate=pl.CostEstimate(flops=8 * work * dim, bytes_accessed=28 << 20, transcendentals=work),
-        compiler_params=pltpu.CompilerParams(dimension_semantics=("arbitrary",), vmem_limit_bytes=62 << 20),
-        name="window_attention",
+        compiler_params=pltpu.CompilerParams(vmem_limit_bytes=62 << 20),
+        name="window",
     )(r0, q, k, v, left, left, right, right, *globs, *globs, bias)
 
 
@@ -157,8 +157,8 @@
         in_specs=[pl.BlockSpec((1, STEP_HEADS, share, dim), lambda h: (2, h, 0, 0))] * len(globs) + [head((n_rows, dim))] * 2,
         out_specs=[head((dim + 8, share))] * len(globs),
         cost_estimate=pl.CostEstimate(flops=8 * work * dim, bytes_accessed=24 << 20, transcendentals=work),
-        compiler_params=pltpu.CompilerParams(dimension_semantics=("arbitrary",), vmem_limit_bytes=62 << 20),
-        name="global_queries",
+        compiler_params=pltpu.CompilerParams(vmem_limit_bytes=62 << 20),
+        name="globals",
     )(*globs, k, v)
 
 
@@ -223,8 +223,8 @@
             scratch_shapes=[pltpu.VMEM((size, heads), BF16), pltpu.VMEM((n_parts, size, part), BF16)],
         ),
         cost_estimate=pl.CostEstimate(flops=4 * size * heads * (width + n_glob), bytes_accessed=40 << 20, transcendentals=0),
-        compiler_params=pltpu.CompilerParams(dimension_semantics=("arbitrary",), vmem_limit_bytes=62 << 20),
-        name="hidden_rows",
+        compiler_params=pltpu.CompilerParams(vmem_limit_bytes=62 << 20),
+        name="hidden",
     )(where, gpos, o_mine, o_other, *globs, *globs, x, wo_mine, *wo_parts)
 
 
@@ -257,9 +257,32 @@
         ],
         out_specs=pl.BlockSpec((size, width), lambda j: (0, 0)),
         cost_estimate=pl.CostEstimate(flops=4 * size * width * inner, bytes_accessed=4 * width * inner, transcendentals=size * inner),
-        compiler_params=pltpu.CompilerParams(dimension_semantics=("arbitrary",), vmem_limit_bytes=62 << 20),
-        name="mlp_rows",
+        compiler_params=pltpu.CompilerParams(vmem_limit_bytes=62 << 20),
+        name="mlp",
     )(h, w_up, w_down)
+
+
+def up_kernel(h_ref, up_ref, u_ref):
+    z = jnp.dot(h_ref[...], up_ref[...], preferred_element_type=F32)
+    u_ref[...] = (0.5 * z * (1.0 + jnp.tanh(math.sqrt(2.0 / math.pi) * (z + 0.044715 * (z * z * z))))).astype(BF16)
+
+
+def down_kernel(u_ref, down_ref, o_ref):
+    o_ref[...] = jnp.dot(u_ref[...], down_ref[...], preferred_element_type=F32)
+
+
+def column_call(kernel, rows, weight, start, stop, tile, dtype):
+    size, depth = rows.shape
+    first = start // tile
+    return pl.pallas_call(
+        kernel,
+        out_shape=jax.ShapeDtypeStruct((size, stop - start), dtype),
+        grid=((stop - start) // tile,),
+        in_specs=[pl.BlockSpec((size, depth), lambda j: (0, 0)), pl.BlockSpec((depth, tile), lambda j: (0, first + j))],
+        out_specs=pl.BlockSpec((size, tile), lambda j: (0, j)),
+        cost_estimate=pl.CostEstimate(flops=2 * size * depth * (stop - start), bytes_accessed=2 * depth * (stop - start), transcendentals=0),
+        compiler_params=pltpu.CompilerParams(vmem_limit_bytes=62 << 20),
+    )(rows, weight)
 
 
 def gate(value, *deps):
@@ -367,18 +390,31 @@
             u = jax.nn.gelu(jnp.dot(h_blk, w_up, preferred_element_type=F32), approximate=True).astype(BF16)
             return lax.optimization_barrier(jnp.dot(u, w_down, preferred_element_type=F32))
 
-        sums, dep = [], att['a1']
-        for key, offset, size in (('a0', 0, 256), ('a0', 256, 256), ('a1', 512, 512)):
-            dep = partial = mlp(hidden_rows(key, away, offset, size, dep))
-            sums.append(lax.ppermute(partial, 'tp', swap))
+        h_blk = hidden_rows('a0', away, 0, 256, att['a1'])
+        u = column_call(up_kernel, h_blk, w_up, 0, w_up.shape[1], 1024, BF16)
+        early = column_call(down_kernel, u, w_down, 0, width // 4, 512, F32)
+        dep = late = column_call(down_kernel, gate(u, early), w_down, width // 4, width, 512, F32)
+        sums = [(lax.ppermute(early, 'tp', swap), lax.ppermute(late, 'tp', swap))]
+        dep = partial = mlp(hidden_rows('a0', away, 256, 256, dep))
+        sums.append(lax.ppermute(partial, 'tp', swap))
+        h_blk = hidden_rows('a1', away, ROWS, ROWS, dep)
+        u = jax.nn.gelu(jnp.dot(h_blk, w_up, preferred_element_type=F32), approximate=True).astype(BF16)
+        early = column_call(down_kernel, u, w_down, 0, width // 2, 512, F32)
+        dep = late = column_call(down_kernel, gate(u, early), w_down, width // 2, width, 512, F32)
+        sums.append((lax.ppermute(early, 'tp', swap), lax.ppermute(late, 'tp', swap)))
 
         def finish(h_blk, partial, total):
             return lax.optimization_barrier((h_blk.astype(F32) + (partial + total)).astype(BF16))
 
         pieces, y_other = [], []
-        for c, arrived in ((0, sums[:2]), (1, [sums[2][:256], sums[2][256:]])):
+        for c in range(2):
             h_blk = hidden_rows('h%d' % c, home, c * ROWS, ROWS, dep)
             dep = partial = mlp(h_blk)
+            if c == 0:
+                arrived = [jnp.concatenate([gate(p, partial) for p in sums[0]], axis=1), sums[1]]
+            else:
+                pair = [gate(p, partial) for p in sums[2]]
+                arrived = [jnp.concatenate([p[i:i + 256] for p in pair], axis=1) for i in (0, 256)]
             size = ROWS // len(arrived)
             for i, total in enumerate(arrived):
                 y = finish(h_blk[i * size:(i + 1) * size], partial[i * size:(i + 1) * size], gate(total, partial))

time: 1060 us -> 1100 us (1.038)
  Pallas kernels: 345 us -> 399 us
  matrix products: 413 us -> 373 us
  waiting for transfers between devices: 203 us -> 238 us
    pallas_call x0 -> x5, Pallas kernels: none -> 100 us  [column_call(): pl.pallas_call(kernel, out_shape=jax.ShapeDtypeStruct((size, stop - start...]
    pallas_call x2 -> x1, Pallas kernels: 91.4 us -> 45.5 us  [mlp_block(): pl.pallas_call(mlp_kernel, out_shape=jax.ShapeDtypeStruct((size, width),...]
    dot_general x0 -> x1, matrix products: none -> 40.6 us  [device_layer(): jnp.dot(h_blk, w_up, preferred_element_type=F32)]
    dot_general x3 -> x2, matrix products: 116 us -> 75.3 us  [mlp(): jnp.dot(u, w_down, preferred_element_type=F32)]
    dot_general x3 -> x2, matrix products: 120 us -> 80.2 us  [mlp(): jnp.dot(h_blk, w_up, preferred_element_type=F32)]
    ppermute x3 -> x1, waiting for transfers between devices: 21.3 us -> 52.3 us  [device_layer(): sums.append(lax.ppermute(partial, 'tp', swap))]
  transfers between devices with their start and end apart: 27 -> 29, of which waited for: 8 -> 7; matrix products, arithmetic and copies ran while one was open for 43% -> 37% of each run, Pallas kernels for 33% -> 36%
where the time goes in v3:
time: 1100 us
  Pallas kernels  399 us (36%)
  matrix products  373 us (34%)
  waiting for transfers between devices  238 us (22%)
  local copies, waits for them, and re-layouts  30.7 us (3%)
  starting transfers between devices  28.7 us (3%)
  other arithmetic  25.9 us (2%)
    dot_general x7, matrix products, project(): jnp.einsum('rd,dhe->hre', rows, weight, preferred_element_type=F32)  164 us
    ppermute x4, waiting for transfers between devices, device_layer(): y_other.append(lax.ppermute(y, 'tp', swap))  161 us
    pallas_call x5, Pallas kernels, hidden_block(): pl.pallas_call(hidden_kernel, out_shape=jax.ShapeDtypeStruct((size, width...  130 us
    pallas_call x5, Pallas kernels, column_call(): pl.pallas_call(kernel, out_shape=jax.ShapeDtypeStruct((size, stop - start...  100 us
    pallas_call x4, Pallas kernels, window_rows(): pl.pallas_call(functools.partial(window_kernel, coef=LOG2E / math.sqrt(di...  90 us
    dot_general x2, matrix products, mlp(): jnp.dot(h_blk, w_up, preferred_element_type=F32)  80.2 us
    dot_general x2, matrix products, mlp(): jnp.dot(u, w_down, preferred_element_type=F32)  75.3 us
    ppermute x1, waiting for transfers between devices, device_layer(): sums.append(lax.ppermute(partial, 'tp', swap))  52.3 us
  transfers between devices with their start and end apart: 29, of which 7 were waited for; matrix products, arithmetic and copies ran while one was open for 37% of the time, Pallas kernels for 36%

profile of v3, /device:TPU:0, one launch (start us, length us, event | category | flops | bytes accessed | tf_op | source)
XLA Modules:
  0.0 1096.6 jit_solution(16676383785393541397)
XLA Ops:
  0.9 12.5 %convolution_convert_fusion = bf16[512,4096]{1,0:T(8,128)(2,1)S(1)} fusion(bf16[2048,4096]{1,0:T(8,128)(2,1)} %refs_8_.9, s32[2048]{0:T(1024)S(1)} %iota_add_fusion.1, s32[512]{0:T(512)S(1)} %pad_add_fusion), kind=kOutput, calls=%fused_computation.59 | convolution fusion | flops 8593080320 | bytes 20981760 | tf_op jit(solution)/shard_map/dot_general | solution.py:317
  13.4 2.0 copy-done.4
  16.4 7.8 constant_dynamic-slice_fusion
  24.2 2.5 collective-permute-start.15
  26.8 1.7 compare_reduce_fusion
  28.5 1.5 broadcast_in_dim.24.refs_8_
  30.0 2.4 slice_add_fusion.4
  33.5 1.5 collective-permute-start.1
  35.0 43.0 %convert_bitcast_fusion.1.k_ref.refs_4_ = bf16[16,2048,128]{2,1,0:T(8,128)(2,1)} fusion(bf16[4096,16,128]{2,1,0:T(8,128)(2,1)} %param.11, bf16[2048,4096]{1,0:T(8,128)(2,1)} %refs_8_.9), kind=kOutput, calls=%fused_computation.48 | convolution fusion | flops 34363932672 | bytes 41943040 | tf_op jit(solution)/shard_map/rd,dhe->hre/dot_general | solution.py:333
  78.2 8.8 fusion.95
  87.0 8.7 fusion.92
  95.8 10.5 fusion.98
  107.0 43.0 %convert_bitcast_fusion.v_ref.refs_5_ = bf16[16,2048,128]{2,1,0:T(8,128)(2,1)} fusion(bf16[4096,16,128]{2,1,0:T(8,128)(2,1)} %param.12, bf16[2048,4096]{1,0:T(8,128)(2,1)} %refs_8_.9), kind=kOutput, calls=%fused_computation.47 | convolution fusion | flops 34363932672 | bytes 41943040 | tf_op jit(solution)/shard_map/rd,dhe->hre/dot_general | solution.py:333
  150.0 2.7 slice_bitcast_fusion
  152.7 1.5 pad_maximum_fusion.3
  154.2 3.4 collective-permute-start.3
  157.6 1.5 pad_maximum_fusion.4
  161.6 25.1 %convert_bitcast_fusion.3.q_ref = bf16[16,1024,128]{2,1,0:T(8,128)(2,1)} fusion(bf16[4096,16,128]{2,1,0:T(8,128)(2,1)} %param.10, bf16[2048,4096]{1,0:T(8,128)(2,1)} %refs_8_.9, s32[]{:T(128)S(6)} %select_n.87), kind=kOutput, calls=%fused_computation.77 | convolution fusion | flops 17181966336 | bytes 29360132 | tf_op jit(solution)/shard_map/rd,dhe->hre/dot_general | solution.py:333
  186.7 22.5 %window.4.om_ref = bf16[512,2048]{1,0:T(8,128)(2,1)} custom-call(s32[1]{0:T(128)} %bitcast.25.r0_ref, bf16[16,1024,128]{2,1,0:T(8,128)(2,1)} %convert_bitcast_fusion.3.q_ref, bf16[16,2048,128]{2,1,0:T(8,128)(2,1)} %convert_bitcast_fusion.1.k_ref.refs_4_, bf16[16,2048,128]{2,1,0:T(8,128)(2,1)} %convert_bitcast_fusion.v_ref.refs_5_, ...), custom_call_target="tpu_custom_call" | custom-call | flops 10737418240 | bytes 29360128 | tf_op jit(solution)/shard_map/window/pallas_call | solution.py:91
  209.5 33.4 %globals.1 = (f32[16,136,128]{2,1,0:T(8,128)}, f32[16,136,128]{2,1,0:T(8,128)}, f32[16,136,128]{2,1,0:T(8,128)}, f32[16,136,128]{2,1,0:T(8,128)}) custom-call(bf16[3,16,128,128]{3,2,1,0:T(8,128)(2,1)} %copy-done, bf16[3,16,128,128]{3,2,1,0:T(8,128)(2,1)} %collective-permute-done.2.refs_1_.refs_5_, ...), custom_call_target="tpu_custom_call" | custom-call | flops 17179869184 | bytes 25165824 | tf_op jit(solution)/shard_map/globals/pallas_call | solution.py:153
  242.9 22.4 %window.5.om_ref = bf16[512,2048]{1,0:T(8,128)(2,1)} custom-call(s32[1]{0:T(128)} %bitcast.32.r0_ref, bf16[16,1024,128]{2,1,0:T(8,128)(2,1)} %convert_bitcast_fusion.3.q_ref, bf16[16,2048,128]{2,1,0:T(8,128)(2,1)} %convert_bitcast_fusion.1.k_ref.refs_4_, bf16[16,2048,128]{2,1,0:T(8,128)(2,1)} %convert_bitcast_fusion.v_ref.refs_5_, ...), custom_call_target="tpu_custom_call" | custom-call | flops 10737418240 | bytes 29360128 | tf_op jit(solution)/shard_map/window/pallas_call | solution.py:91
  265.3 1.8 collective-permute-start.7
  267.6 25.3 %convert_bitcast_fusion.2.q_ref = bf16[16,1024,128]{2,1,0:T(8,128)(2,1)} fusion(bf16[4096,16,128]{2,1,0:T(8,128)(2,1)} %param.10, bf16[2048,4096]{1,0:T(8,128)(2,1)} %refs_8_.9, s32[]{:T(128)S(6)} %select_n.88), kind=kOutput, calls=%fused_computation.76 | convolution fusion | flops 17181966336 | bytes 29360132 | tf_op jit(solution)/shard_map/rd,dhe->hre/dot_general | solution.py:333
  293.0 22.8 %collective-permute-done.9 = f32[16,136,128]{2,1,0:T(8,128)S(1)} collective-permute-done((f32[16,136,128]{2,1,0:T(8,128)}, f32[16,136,128]{2,1,0:T(8,128)S(1)}, u32[]{:S(2)}, u32[]{:S(2)}) %collective-permute-start.9) | collective-permute-done | bytes 1114144 | tf_op jit(solution)/shard_map/ppermute | solution.py:364
  316.8 1.6 fusion.102
  318.4 1.3 collective-permute-start.11
  319.8 22.6 %window.6.om_ref = bf16[512,2048]{1,0:T(8,128)(2,1)} custom-call(s32[1]{0:T(128)} %bitcast.13.r0_ref, bf16[16,1024,128]{2,1,0:T(8,128)(2,1)} %convert_bitcast_fusion.2.q_ref, bf16[16,2048,128]{2,1,0:T(8,128)(2,1)} %convert_bitcast_fusion.1.k_ref.refs_4_, bf16[16,2048,128]{2,1,0:T(8,128)(2,1)} %convert_bitcast_fusion.v_ref.refs_5_, ...), custom_call_target="tpu_custom_call" | custom-call | flops 10737418240 | bytes 29360128 | tf_op jit(solution)/shard_map/window/pallas_call | solution.py:91
  345.4 22.5 %window.7.om_ref = bf16[512,2048]{1,0:T(8,128)(2,1)} custom-call(s32[1]{0:T(128)} %bitcast.12.r0_ref, bf16[16,1024,128]{2,1,0:T(8,128)(2,1)} %convert_bitcast_fusion.2.q_ref, bf16[16,2048,128]{2,1,0:T(8,128)(2,1)} %convert_bitcast_fusion.1.k_ref.refs_4_, bf16[16,2048,128]{2,1,0:T(8,128)(2,1)} %convert_bitcast_fusion.v_ref.refs_5_, ...), custom_call_target="tpu_custom_call" | custom-call | flops 10737418240 | bytes 29360128 | tf_op jit(solution)/shard_map/window/pallas_call | solution.py:91
  368.2 1.6 collective-permute-done.12.refs_1_.refs_5_
  372.8 1.5 collective-permute-start.19
  375.8 21.5 %hidden.5.h_ref = bf16[256,4096]{1,0:T(8,128)(2,1)} custom-call(s32[4]{0:T(128)} %add_add_fusion.4.where_ref, s32[1,512]{1,0:T(1,128)} %bitcast.124, bf16[512,2048]{1,0:T(8,128)(2,1)} %window.6.om_ref, bf16[512,2048]{1,0:T(8,128)(2,1)} %collective-permute-done.10.oo_ref, bf16[2,2048,128]{2,1,0:T(8,128)(2,1)} %copy-done.1, ...), custom_call_target="tpu_custom_call" | custom-call | flops 9663676416 | bytes 41943040 | tf_op jit(solution)/shard_map/hidden/pallas_call | solution.py:207
  397.3 26.3 %shard_map.82.u_ref = bf16[256,7168]{1,0:T(8,128)(2,1)} custom-call(bf16[256,4096]{1,0:T(8,128)(2,1)} %hidden.5.h_ref, bf16[4096,7168]{1,0:T(8,128)(2,1)} %up_ref.3), custom_call_target="tpu_custom_call" | custom-call | flops 15032385536 | bytes 58720256 | tf_op jit(solution)/shard_map/pallas_call | solution.py:277
  423.6 9.1 shard_map.83
  432.7 1.5 collective-permute-start.20
  434.2 20.5 %shard_map.84 = f32[256,3072]{1,0:T(8,128)} custom-call(bf16[256,7168]{1,0:T(8,128)(2,1)} %shard_map.82.u_ref, bf16[7168,4096]{1,0:T(8,128)(2,1)} %down_ref.9), custom_call_target="tpu_custom_call" | custom-call | flops 11274289152 | bytes 44040192 | tf_op jit(solution)/shard_map/pallas_call | solution.py:277
  455.2 21.5 %hidden.6.h_ref = bf16[256,4096]{1,0:T(8,128)(2,1)} custom-call(s32[4]{0:T(128)} %add_add_fusion.3.where_ref, s32[1,512]{1,0:T(1,128)} %bitcast.125, bf16[512,2048]{1,0:T(8,128)(2,1)} %window.6.om_ref, bf16[512,2048]{1,0:T(8,128)(2,1)} %collective-permute-done.10.oo_ref, bf16[2,2048,128]{2,1,0:T(8,128)(2,1)} %copy-done.1, ...), custom_call_target="tpu_custom_call" | custom-call | flops 9663676416 | bytes 41943040 | tf_op jit(solution)/shard_map/hidden/pallas_call | solution.py:207
  476.7 45.5 %mlp.1 = f32[256,4096]{1,0:T(8,128)} custom-call(bf16[256,4096]{1,0:T(8,128)(2,1)} %hidden.6.h_ref, bf16[4096,7168]{1,0:T(8,128)(2,1)} %up_ref.3, bf16[7168,4096]{1,0:T(8,128)(2,1)} %down_ref.9), custom_call_target="tpu_custom_call" | custom-call | flops 30064771072 | bytes 117440512 | tf_op jit(solution)/shard_map/mlp/pallas_call | solution.py:249
  522.3 29.2 %hidden.7 = bf16[512,4096]{1,0:T(8,128)(2,1)} custom-call(s32[4]{0:T(128)} %add_add_fusion.2.where_ref, s32[1,512]{1,0:T(1,128)} %bitcast.126, bf16[512,2048]{1,0:T(8,128)(2,1)} %window.7.om_ref, bf16[512,2048]{1,0:T(8,128)(2,1)} %collective-permute-done.17.oo_ref, bf16[2,2048,128]{2,1,0:T(8,128)(2,1)} %copy-done.1, ...), custom_call_target="tpu_custom_call" | custom-call | flops 19327352832 | bytes 41943040 | tf_op jit(solution)/shard_map/hidden/pallas_call | solution.py:207
  551.4 40.6 %fusion.17.u_ref = bf16[512,7168]{1,0:T(8,128)(2,1)} fusion(bf16[512,4096]{1,0:T(8,128)(2,1)} %hidden.7, bf16[4096,7168]{1,0:T(8,128)(2,1)} %up_ref.3), kind=kOutput, calls=%fused_computation.20 | convolution fusion | flops 30097801216 | bytes 70254592 | tf_op jit(solution)/shard_map/dot_general | solution.py:401
  592.0 22.0 %shard_map.85 = f32[512,2048]{1,0:T(8,128)} custom-call(bf16[512,7168]{1,0:T(8,128)(2,1)} %fusion.17.u_ref, bf16[7168,4096]{1,0:T(8,128)(2,1)} %down_ref.9), custom_call_target="tpu_custom_call" | custom-call | flops 15032385536 | bytes 29360128 | tf_op jit(solution)/shard_map/pallas_call | solution.py:277
  614.1 22.2 %shard_map.86 = f32[512,2048]{1,0:T(8,128)} custom-call(bf16[512,7168]{1,0:T(8,128)(2,1)} %fusion.17.u_ref, bf16[7168,4096]{1,0:T(8,128)(2,1)} %down_ref.9), custom_call_target="tpu_custom_call" | custom-call | flops 15032385536 | bytes 29360128 | tf_op jit(solution)/shard_map/pallas_call | solution.py:277
  636.3 1.5 collective-permute-start.24
  638.3 28.8 %hidden.8 = bf16[512,4096]{1,0:T(8,128)(2,1)} custom-call(s32[4]{0:T(128)} %get-tuple-element.64.where_ref, s32[1,512]{1,0:T(1,128)} %bitcast.127, bf16[512,2048]{1,0:T(8,128)(2,1)} %window.4.om_ref, bf16[512,2048]{1,0:T(8,128)(2,1)} %collective-permute-done.18.oo_ref, bf16[2,2048,128]{2,1,0:T(8,128)(2,1)} %copy-done.1, ...), custom_call_target="tpu_custom_call" | custom-call | flops 19327352832 | bytes 41943040 | tf_op jit(solution)/shard_map/hidden/pallas_call | solution.py:207
  667.1 39.4 %fusion.149 = bf16[512,7168]{1,0:T(8,128)(2,1)S(1)} fusion(bf16[512,4096]{1,0:T(8,128)(2,1)} %hidden.8, bf16[4096,7168]{1,0:T(8,128)(2,1)} %up_ref.3), kind=kOutput, calls=%fused_computation.28.clone.clone | convolution fusion | flops 30097801216 | bytes 70254592 | tf_op jit(solution)/shard_map/dot_general | solution.py:390
  706.5 38.2 %fusion.46 = f32[512,4096]{1,0:T(8,128)} fusion(bf16[7168,4096]{1,0:T(8,128)(2,1)} %down_ref.9, bf16[512,7168]{1,0:T(8,128)(2,1)S(1)} %fusion.149), kind=kOutput, calls=%fused_computation.50 | convolution fusion | flops 30064771072 | bytes 74448896 | tf_op jit(solution)/shard_map/dot_general | solution.py:391
  744.6 1.5 collective-permute-start.22
  746.1 28.8 %hidden.9 = bf16[512,4096]{1,0:T(8,128)(2,1)} custom-call(s32[4]{0:T(128)} %get-tuple-element.65.where_ref, s32[1,512]{1,0:T(1,128)} %bitcast.128, bf16[512,2048]{1,0:T(8,128)(2,1)} %window.5.om_ref, bf16[512,2048]{1,0:T(8,128)(2,1)} %collective-permute-done.19.oo_ref, bf16[2,2048,128]{2,1,0:T(8,128)(2,1)} %copy-done.1, ...), custom_call_target="tpu_custom_call" | custom-call | flops 19327352832 | bytes 41943040 | tf_op jit(solution)/shard_map/hidden/pallas_call | solution.py:207
  774.9 40.9 %fusion.145 = bf16[512,7168]{1,0:T(8,128)(2,1)} fusion(bf16[512,4096]{1,0:T(8,128)(2,1)} %hidden.9, bf16[4096,7168]{1,0:T(8,128)(2,1)} %up_ref.3), kind=kOutput, calls=%fused_computation.36.clone.clone.1 | convolution fusion | flops 30097801216 | bytes 70254592 | tf_op jit(solution)/shard_map/dot_general | solution.py:390
  815.8 37.2 %fusion.44 = f32[512,4096]{1,0:T(8,128)S(1)} fusion(bf16[7168,4096]{1,0:T(8,128)(2,1)} %down_ref.9, bf16[512,7168]{1,0:T(8,128)(2,1)} %fusion.145), kind=kOutput, calls=%fused_computation.49 | convolution fusion | flops 30064771072 | bytes 74448896 | tf_op jit(solution)/shard_map/dot_general | solution.py:391
  853.0 2.6 pad_maximum_fusion
  855.6 52.3 %collective-permute-done.22 = f32[256,4096]{1,0:T(8,128)} collective-permute-done((f32[256,4096]{1,0:T(8,128)}, f32[256,4096]{1,0:T(8,128)}, u32[]{:S(2)}, u32[]{:S(2)}) %collective-permute-start.22) | collective-permute-done | bytes 4194336 | tf_op jit(solution)/shard_map/ppermute | solution.py:399
  908.0 6.0 fusion.69
  914.0 1.5 collective-permute-start.25
  916.1 2.6 fusion.120
  918.7 2.6 fusion.119
  922.0 3.7 fusion.65
  925.7 1.5 collective-permute-start.27
  927.8 1.9 broadcast_in_dim.12
  930.8 31.9 %collective-permute-done.25 = bf16[256,4096]{1,0:T(8,128)(2,1)} collective-permute-done((bf16[256,4096]{1,0:T(8,128)(2,1)S(1)}, bf16[256,4096]{1,0:T(8,128)(2,1)}, u32[]{:S(2)}, u32[]{:S(2)}) %collective-permute-start.25) | collective-permute-done | bytes 2097184 | tf_op jit(solution)/shard_map/ppermute | solution.py:421
  962.7 1.9 constant_dynamic-update-slice_fusion.3
  964.5 43.0 %collective-permute-done.26 = bf16[256,4096]{1,0:T(8,128)(2,1)S(1)} collective-permute-done((bf16[256,4096]{1,0:T(8,128)(2,1)S(1)}, bf16[256,4096]{1,0:T(8,128)(2,1)S(1)}, u32[]{:S(2)}, u32[]{:S(2)}) %collective-permute-start.26) | collective-permute-done | bytes 2097184 | tf_op jit(solution)/shard_map/ppermute | solution.py:421
  1007.8 44.7 %collective-permute-done.27 = bf16[256,4096]{1,0:T(8,128)(2,1)S(1)} collective-permute-done((bf16[256,4096]{1,0:T(8,128)(2,1)S(1)}, bf16[256,4096]{1,0:T(8,128)(2,1)S(1)}, u32[]{:S(2)}, u32[]{:S(2)}) %collective-permute-start.27) | collective-permute-done | bytes 2097184 | tf_op jit(solution)/shard_map/ppermute | solution.py:421
  1052.7 41.9 %collective-permute-done.28 = bf16[256,4096]{1,0:T(8,128)(2,1)S(1)} collective-permute-done((bf16[256,4096]{1,0:T(8,128)(2,1)S(1)}, bf16[256,4096]{1,0:T(8,128)(2,1)S(1)}, u32[]{:S(2)}, u32[]{:S(2)}) %collective-permute-start.28) | collective-permute-done | bytes 2097184 | tf_op jit(solution)/shard_map/ppermute | solution.py:421
  1094.7 1.5 constant_dynamic-update-slice_fusion
  (95 shorter events, 20.3 us)
Async XLA Ops:
  0.9 12.5 %copy-start.9 = (s32[512]{0:T(512)}, s32[512]{0:T(512)S(1)}, u32[]{:S(2)}) copy-start(s32[512]{0:T(512)S(1)} %pad_add_fusion) | copy-start | bytes 6148
  13.4 2.0 copy-start.4
  15.6 14.4 %collective-permute-start = (bf16[256,4096]{1,0:T(8,128)(2,1)S(1)}, bf16[256,4096]{1,0:T(8,128)(2,1)}, u32[]{:S(2)}, u32[]{:S(2)}) collective-permute-start(bf16[256,4096]{1,0:T(8,128)(2,1)S(1)} %slice.129), channel_id=1, source_target_pairs={{0,1},{1,0},{2,3},{3,2},{4,5},{5,4},{6,7},{7,6}} | collective-permute-start | bytes 6291464 | tf_op jit(solution)/shard_map/ppermute | solution.py:319
  16.4 10.3 copy-start.10
  24.2 243.2 %collective-permute-start.15 = (bf16[1024,4096]{1,0:T(8,128)(2,1)}, bf16[1024,4096]{1,0:T(8,128)(2,1)}, u32[]{:S(2)}, u32[]{:S(2)}) collective-permute-start(bf16[1024,4096]{1,0:T(8,128)(2,1)} %constant_dynamic-slice_fusion), channel_id=1, source_target_pairs={{0,4},{4,0},{1,5},{5,1},{2,6},{6,2},{3,7},{7,3}} | collective-permute-start | bytes 25165832 | tf_op jit(solution)/shard_map/ppermute | solution.py:324
  33.5 44.5 %collective-permute-start.1 = (bf16[128,4096]{1,0:T(8,128)(2,1)}, bf16[128,4096]{1,0:T(8,128)(2,1)S(1)}, u32[]{:S(2)}, u32[]{:S(2)}) collective-permute-start(bf16[128,4096]{1,0:T(8,128)(2,1)} %slice.131), channel_id=1, source_target_pairs={{0,2},{1,3},{2,0},{3,1},{4,6},{5,7},{6,4},{7,5}} | collective-permute-start | bytes 3145736 | tf_op jit(solution)/shard_map/ppermute | solution.py:320
  78.1 17.6 %slice-start = ((s8[16777216]{0:T(1024)(128)(4,1)}), s8[4194304]{0:T(1024)(128)(4,1)S(1)}, s32[]{:S(2)}) async-start(s8[16777216]{0:T(1024)(128)(4,1)} %bitcast.129), calls=%async_computation | async-start | bytes 8388608
  78.1 17.6 %slice-start.1 = ((s8[16777216]{0:T(1024)(128)(4,1)}), s8[4194304]{0:T(1024)(128)(4,1)S(1)}, s32[]{:S(2)}) async-start(s8[16777216]{0:T(1024)(128)(4,1)} %bitcast.129), calls=%async_computation.1 | async-start | bytes 8388608
  78.2 17.6 %slice-start.2 = ((s8[16777216]{0:T(1024)(128)(4,1)}), s8[4194304]{0:T(1024)(128)(4,1)S(1)}, s32[]{:S(2)}) async-start(s8[16777216]{0:T(1024)(128)(4,1)} %bitcast.129), calls=%async_computation.2 | async-start | bytes 8388608
  87.0 8.7 slice-start.3
  106.5 43.6 %copy-start = (bf16[3,16,128,128]{3,2,1,0:T(8,128)(2,1)}, bf16[3,16,128,128]{3,2,1,0:T(8,128)(2,1)S(1)}, u32[]{:S(2)}) copy-start(bf16[3,16,128,128]{3,2,1,0:T(8,128)(2,1)S(1)} %pad_maximum_fusion.5.refs_0_.refs_4_) | copy-start | bytes 4718596
  106.5 80.2 %collective-permute-start.5 = (bf16[3,16,128,128]{3,2,1,0:T(8,128)(2,1)S(1)}, bf16[3,16,128,128]{3,2,1,0:T(8,128)(2,1)}, u32[]{:S(2)}, u32[]{:S(2)}) collective-permute-start(bf16[3,16,128,128]{3,2,1,0:T(8,128)(2,1)S(1)} %pad_maximum_fusion.5.refs_0_.refs_4_), channel_id=1, source_target_pairs={{0,1},{1,0},{2,3},{3,2},{4,5},{5,4},{6,7},{7,6}} | collective-permute-start | bytes 4718600 | tf_op jit(solution)/shard_map/ppermute | solution.py:339
  106.5 53.9 %collective-permute-start.2 = (bf16[3,16,128,128]{3,2,1,0:T(8,128)(2,1)S(1)}, bf16[3,16,128,128]{3,2,1,0:T(8,128)(2,1)}, u32[]{:S(2)}, u32[]{:S(2)}) collective-permute-start(bf16[3,16,128,128]{3,2,1,0:T(8,128)(2,1)S(1)} %pad_maximum_fusion.5.refs_0_.refs_4_), channel_id=1, source_target_pairs={{0,2},{1,3},{2,0},{3,1},{4,6},{5,7},{6,4},{7,5}} | collective-permute-start | bytes 4718600 | tf_op jit(solution)/shard_map/ppermute | solution.py:338
  154.2 32.5 %collective-permute-start.3 = (bf16[2,16,256,128]{3,2,1,0:T(8,128)(2,1)}, bf16[2,16,256,128]{3,2,1,0:T(8,128)(2,1)}, u32[]{:S(2)}, u32[]{:S(2)}) collective-permute-start(bf16[2,16,256,128]{3,2,1,0:T(8,128)(2,1)} %pad_maximum_fusion.3), channel_id=1, source_target_pairs={{0,1},{1,2},{2,3},{4,5},{5,6},{6,7}} | collective-permute-start | bytes 6291464 | tf_op jit(solution)/shard_map/ppermute | solution.py:341
  159.1 27.6 %collective-permute-start.4 = (bf16[2,16,256,128]{3,2,1,0:T(8,128)(2,1)}, bf16[2,16,256,128]{3,2,1,0:T(8,128)(2,1)}, u32[]{:S(2)}, u32[]{:S(2)}) collective-permute-start(bf16[2,16,256,128]{3,2,1,0:T(8,128)(2,1)} %pad_maximum_fusion.4), channel_id=1, source_target_pairs={{1,0},{2,1},{3,2},{5,4},{6,5},{7,6}} | collective-permute-start | bytes 6291464 | tf_op jit(solution)/shard_map/ppermute | solution.py:342
  160.4 26.3 %collective-permute-start.6 = (bf16[3,16,128,128]{3,2,1,0:T(8,128)(2,1)}, bf16[3,16,128,128]{3,2,1,0:T(8,128)(2,1)}, u32[]{:S(2)}, u32[]{:S(2)}) collective-permute-start(bf16[3,16,128,128]{3,2,1,0:T(8,128)(2,1)} %collective-permute-done.2.refs_1_.refs_5_), channel_id=1, source_target_pairs={{0,1},{1,0},{2,3},{3,2},{4,5},{5,4},{6,7},{7,6}} | collective-permute-start | bytes 4718600 | tf_op jit(solution)/shard_map/ppermute | solution.py:344
  209.2 163.6 %collective-permute-start.10 = (bf16[512,2048]{1,0:T(8,128)(2,1)}, bf16[512,2048]{1,0:T(8,128)(2,1)}, u32[]{:S(2)}, u32[]{:S(2)}) collective-permute-start(bf16[512,2048]{1,0:T(8,128)(2,1)} %window.4.om_ref), channel_id=1, source_target_pairs={{0,4},{4,0},{1,5},{5,1},{2,6},{6,2},{3,7},{7,3}} | collective-permute-start | bytes 6291464 | tf_op jit(solution)/shard_map/ppermute | solution.py:358
  265.3 27.7 %collective-permute-start.7 = (f32[16,136,128]{2,1,0:T(8,128)}, f32[16,136,128]{2,1,0:T(8,128)S(1)}, u32[]{:S(2)}, u32[]{:S(2)}) collective-permute-start(f32[16,136,128]{2,1,0:T(8,128)} %get-tuple-element.52), channel_id=1, source_target_pairs={{0,2},{1,3},{2,0},{3,1},{4,6},{5,7},{6,4},{7,5}} | collective-permute-start | bytes 3342344 | tf_op jit(solution)/shard_map/ppermute | solution.py:364
  267.1 25.9 %collective-permute-start.8 = (f32[16,136,128]{2,1,0:T(8,128)}, f32[16,136,128]{2,1,0:T(8,128)S(1)}, u32[]{:S(2)}, u32[]{:S(2)}) collective-permute-start(f32[16,136,128]{2,1,0:T(8,128)} %get-tuple-element.53), channel_id=1, source_target_pairs={{0,1},{1,0},{2,3},{3,2},{4,5},{5,4},{6,7},{7,6}} | collective-permute-start | bytes 3342344 | tf_op jit(solution)/shard_map/ppermute | solution.py:364
  267.1 48.7 %collective-permute-start.9 = (f32[16,136,128]{2,1,0:T(8,128)}, f32[16,136,128]{2,1,0:T(8,128)S(1)}, u32[]{:S(2)}, u32[]{:S(2)}) collective-permute-start(f32[16,136,128]{2,1,0:T(8,128)} %get-tuple-element.54), channel_id=1, source_target_pairs={{0,3},{1,2},{2,1},{3,0},{4,7},{5,6},{6,5},{7,4}} | collective-permute-start | bytes 3342344 | tf_op jit(solution)/shard_map/ppermute | solution.py:364
  267.5 48.3 %copy-start.7 = (f32[16,136,128]{2,1,0:T(8,128)S(1)}, f32[16,136,128]{2,1,0:T(8,128)}, u32[]{:S(2)}) copy-start(f32[16,136,128]{2,1,0:T(8,128)} %get-tuple-element.51) | copy-start | bytes 3342340
  267.5 108.3 %collective-permute-start.16 = (bf16[1024,4096]{1,0:T(8,128)(2,1)}, bf16[1024,4096]{1,0:T(8,128)(2,1)}, u32[]{:S(2)}, u32[]{:S(2)}) collective-permute-start(bf16[1024,4096]{1,0:T(8,128)(2,1)} %collective-permute-done.15.refs_10_), channel_id=1, source_target_pairs={{0,1},{1,0},{2,3},{3,2},{4,5},{5,4},{6,7},{7,6}} | collective-permute-start | bytes 25165832 | tf_op jit(solution)/shard_map/ppermute | solution.py:325
  315.8 1.0 copy-start.6
  318.4 24.0 %collective-permute-start.11 = (bf16[2048,128]{1,0:T(8,128)(2,1)S(1)}, bf16[2048,128]{1,0:T(8,128)(2,1)S(1)}, u32[]{:S(2)}, u32[]{:S(2)}) collective-permute-start(bf16[2048,128]{1,0:T(8,128)(2,1)S(1)} %bitcast.113), channel_id=1, source_target_pairs={{0,4},{4,0},{1,5},{5,1},{2,6},{6,2},{3,7},{7,3}} | collective-permute-start | bytes 1572872 | tf_op jit(solution)/shard_map/ppermute | solution.py:369
  342.4 0.8 copy-start.8
  344.3 23.5 %copy-start.1 = (bf16[2,2048,128]{2,1,0:T(8,128)(2,1)}, bf16[2,2048,128]{2,1,0:T(8,128)(2,1)S(1)}, u32[]{:S(2)}) copy-start(bf16[2,2048,128]{2,1,0:T(8,128)(2,1)S(1)} %pad_maximum_fusion.6.refs_0_.refs_4_) | copy-start | bytes 3145732
  344.4 25.5 %collective-permute-start.12 = (bf16[2,2048,128]{2,1,0:T(8,128)(2,1)S(1)}, bf16[2,2048,128]{2,1,0:T(8,128)(2,1)}, u32[]{:S(2)}, u32[]{:S(2)}) collective-permute-start(bf16[2,2048,128]{2,1,0:T(8,128)(2,1)S(1)} %pad_maximum_fusion.6.refs_0_.refs_4_), channel_id=1, source_target_pairs={{0,2},{1,3},{2,0},{3,1},{4,6},{5,7},{6,4},{7,5}} | collective-permute-start | bytes 3145736 | tf_op jit(solution)/shard_map/ppermute | solution.py:373
  367.9 6.4 collective-permute-start.13
  369.8 6.0 collective-permute-start.14
  372.3 150.0 %collective-permute-start.17 = (bf16[512,2048]{1,0:T(8,128)(2,1)}, bf16[512,2048]{1,0:T(8,128)(2,1)}, u32[]{:S(2)}, u32[]{:S(2)}) collective-permute-start(bf16[512,2048]{1,0:T(8,128)(2,1)} %window.5.om_ref), channel_id=1, source_target_pairs={{0,4},{4,0},{1,5},{5,1},{2,6},{6,2},{3,7},{7,3}} | collective-permute-start | bytes 6291464 | tf_op jit(solution)/shard_map/ppermute | solution.py:366
  372.8 371.8 %collective-permute-start.19 = (bf16[512,2048]{1,0:T(8,128)(2,1)}, bf16[512,2048]{1,0:T(8,128)(2,1)}, u32[]{:S(2)}, u32[]{:S(2)}) collective-permute-start(bf16[512,2048]{1,0:T(8,128)(2,1)} %window.7.om_ref), channel_id=1, source_target_pairs={{0,4},{4,0},{1,5},{5,1},{2,6},{6,2},{3,7},{7,3}} | collective-permute-start | bytes 6291464 | tf_op jit(solution)/shard_map/ppermute | solution.py:376
  374.3 1.0 copy-start.2
  375.3 262.5 %collective-permute-start.18 = (bf16[512,2048]{1,0:T(8,128)(2,1)}, bf16[512,2048]{1,0:T(8,128)(2,1)}, u32[]{:S(2)}, u32[]{:S(2)}) collective-permute-start(bf16[512,2048]{1,0:T(8,128)(2,1)} %window.6.om_ref), channel_id=1, source_target_pairs={{0,4},{4,0},{1,5},{5,1},{2,6},{6,2},{3,7},{7,3}} | collective-permute-start | bytes 6291464 | tf_op jit(solution)/shard_map/ppermute | solution.py:371
  432.7 420.3 %collective-permute-start.20 = (f32[256,1024]{1,0:T(8,128)}, f32[256,1024]{1,0:T(8,128)}, u32[]{:S(2)}, u32[]{:S(2)}) collective-permute-start(f32[256,1024]{1,0:T(8,128)} %shard_map.83), channel_id=1, source_target_pairs={{0,4},{4,0},{1,5},{5,1},{2,6},{6,2},{3,7},{7,3}} | collective-permute-start | bytes 3145736 | tf_op jit(solution)/shard_map/ppermute | solution.py:397
  454.7 398.3 %collective-permute-start.21 = (f32[256,3072]{1,0:T(8,128)}, f32[256,3072]{1,0:T(8,128)}, u32[]{:S(2)}, u32[]{:S(2)}) collective-permute-start(f32[256,3072]{1,0:T(8,128)} %shard_map.84), channel_id=1, source_target_pairs={{0,4},{4,0},{1,5},{5,1},{2,6},{6,2},{3,7},{7,3}} | collective-permute-start | bytes 9437192 | tf_op jit(solution)/shard_map/ppermute | solution.py:397
  636.3 279.8 %collective-permute-start.24 = (f32[512,2048]{1,0:T(8,128)}, f32[512,2048]{1,0:T(8,128)}, u32[]{:S(2)}, u32[]{:S(2)}) collective-permute-start(f32[512,2048]{1,0:T(8,128)} %shard_map.86), channel_id=1, source_target_pairs={{0,4},{4,0},{1,5},{5,1},{2,6},{6,2},{3,7},{7,3}} | collective-permute-start | bytes 12582920 | tf_op jit(solution)/shard_map/ppermute | solution.py:404
  637.8 280.9 %collective-permute-start.23 = (f32[512,2048]{1,0:T(8,128)}, f32[512,2048]{1,0:T(8,128)}, u32[]{:S(2)}, u32[]{:S(2)}) collective-permute-start(f32[512,2048]{1,0:T(8,128)} %shard_map.85), channel_id=1, source_target_pairs={{0,4},{4,0},{1,5},{5,1},{2,6},{6,2},{3,7},{7,3}} | collective-permute-start | bytes 12582920 | tf_op jit(solution)/shard_map/ppermute | solution.py:404
  744.6 163.3 %collective-permute-start.22 = (f32[256,4096]{1,0:T(8,128)}, f32[256,4096]{1,0:T(8,128)}, u32[]{:S(2)}, u32[]{:S(2)}) collective-permute-start(f32[256,4096]{1,0:T(8,128)} %mlp.1), channel_id=1, source_target_pairs={{0,4},{4,0},{1,5},{5,1},{2,6},{6,2},{3,7},{7,3}} | collective-permute-start | bytes 12582920 | tf_op jit(solution)/shard_map/ppermute | solution.py:399
  853.0 55.0 %copy-start.5 = (bf16[512,4096]{1,0:T(8,128)(2,1)S(1)}, bf16[512,4096]{1,0:T(8,128)(2,1)}, u32[]{:S(2)}) copy-start(bf16[512,4096]{1,0:T(8,128)(2,1)} %hidden.8) | copy-start | bytes 12582916
  914.0 48.6 %collective-permute-start.25 = (bf16[256,4096]{1,0:T(8,128)(2,1)S(1)}, bf16[256,4096]{1,0:T(8,128)(2,1)}, u32[]{:S(2)}, u32[]{:S(2)}) collective-permute-start(bf16[256,4096]{1,0:T(8,128)(2,1)S(1)} %get-tuple-element.89), channel_id=1, source_target_pairs={{0,4},{4,0},{1,5},{5,1},{2,6},{6,2},{3,7},{7,3}} | collective-permute-start | bytes 6291464 | tf_op jit(solution)/shard_map/ppermute | solution.py:421
  915.5 91.9 %collective-permute-start.26 = (bf16[256,4096]{1,0:T(8,128)(2,1)S(1)}, bf16[256,4096]{1,0:T(8,128)(2,1)S(1)}, u32[]{:S(2)}, u32[]{:S(2)}) collective-permute-start(bf16[256,4096]{1,0:T(8,128)(2,1)S(1)} %get-tuple-element.88), channel_id=1, source_target_pairs={{0,4},{4,0},{1,5},{5,1},{2,6},{6,2},{3,7},{7,3}} | collective-permute-start | bytes 6291464 | tf_op jit(solution)/shard_map/ppermute | solution.py:421
  925.7 126.7 %collective-permute-start.27 = (bf16[256,4096]{1,0:T(8,128)(2,1)S(1)}, bf16[256,4096]{1,0:T(8,128)(2,1)S(1)}, u32[]{:S(2)}, u32[]{:S(2)}) collective-permute-start(bf16[256,4096]{1,0:T(8,128)(2,1)S(1)} %get-tuple-element.87), channel_id=1, source_target_pairs={{0,4},{4,0},{1,5},{5,1},{2,6},{6,2},{3,7},{7,3}} | collective-permute-start | bytes 6291464 | tf_op jit(solution)/shard_map/ppermute | solution.py:421
  927.2 167.4 %collective-permute-start.28 = (bf16[256,4096]{1,0:T(8,128)(2,1)S(1)}, bf16[256,4096]{1,0:T(8,128)(2,1)S(1)}, u32[]{:S(2)}, u32[]{:S(2)}) collective-permute-start(bf16[256,4096]{1,0:T(8,128)(2,1)S(1)} %get-tuple-element.86), channel_id=1, source_target_pairs={{0,4},{4,0},{1,5},{5,1},{2,6},{6,2},{3,7},{7,3}} | collective-permute-start | bytes 6291464 | tf_op jit(solution)/shard_map/ppermute | solution.py:421
  1052.7 42.0 %copy-start.3 = (bf16[2048,4096]{1,0:T(8,128)(2,1)}, bf16[2048,4096]{1,0:T(8,128)(2,1)S(1)}, u32[]{:S(2)}) copy-start(bf16[2048,4096]{1,0:T(8,128)(2,1)S(1)} %constant_dynamic-update-slice_fusion.1) | copy-start | bytes 50331652
